TPU v7x, 16 devices: a whole 2x2x2 slice. The times are simulated.
16 devices in a mesh: fsdp: 16 (over z, y, x, core).
Axes of the slice: x: 2, y: 2, z: 2, core: 2. Of those that a mesh axis runs over, the one named last changes fastest.
Arguments:
- w_query: float32 [2, 960, 960], P(None, 'fsdp')
- w_key: float32 [2, 960, 320], P(None, 'fsdp')
- w_value: float32 [2, 960, 320], P(None, 'fsdp')
- w_out: float32 [2, 960, 960], P(None, 'fsdp')
- w_gate: float32 [2, 960, 2560], P(None, 'fsdp')
- w_up: float32 [2, 960, 2560], P(None, 'fsdp')
- w_down: float32 [2, 2560, 960], P(None, 'fsdp')
- gain_attn: float32 [2, 960], P(None, 'fsdp')
- gain_mlp: float32 [2, 960], P(None, 'fsdp')
- rope_cos: float32 [256, 32], replicated
- rope_sin: float32 [256, 32], replicated
- x_in: bfloat16 [256, 256, 960], P('fsdp')
- y_cot: bfloat16 [256, 256, 960], P('fsdp')
Outputs:
- output 1: bfloat16 [256, 256, 960], P('fsdp')
- output 2: bfloat16 [256, 256, 960], P('fsdp')
- output 3: float32 [2, 960, 960], P(None, 'fsdp')
- output 4: float32 [2, 960, 320], P(None, 'fsdp')
- output 5: float32 [2, 960, 320], P(None, 'fsdp')
- output 6: float32 [2, 960, 960], P(None, 'fsdp')
- output 7: float32 [2, 960, 2560], P(None, 'fsdp')
- output 8: float32 [2, 960, 2560], P(None, 'fsdp')
- output 9: float32 [2, 2560, 960], P(None, 'fsdp')
- output 10: float32 [2, 960], P(None, 'fsdp')
- output 11: float32 [2, 960], P(None, 'fsdp')
All inputs are finite; a program needn't handle non-finite values.
Results may differ from a plain program's by a relative error of at most 0.02.
Values are sent between devices in bfloat16 or wider.
A program may use at most 1 GiB of HBM per device.

v0:
```python
import jax
import jax.numpy as jnp
from jax import lax
from jax.sharding import PartitionSpec as P

NORM_EPS = 1e-5
MASK_VALUE = -1e30


def rms_forward(values, gain):
    vals32 = values.astype(jnp.float32)
    inv_rms = lax.rsqrt(jnp.mean(vals32 * vals32, axis=-1, keepdims=True) + NORM_EPS)
    normed = (vals32 * inv_rms * gain.astype(jnp.float32)).astype(jnp.bfloat16)
    return normed, inv_rms


def rms_backward(values, inv_rms, gain, grad_normed):
    scaled = values.astype(jnp.float32) * inv_rms
    grad_scaled = grad_normed * gain.astype(jnp.float32)
    grad_gain = jnp.sum(grad_normed * scaled, axis=(0, 1))
    grad_values = inv_rms * (grad_scaled - scaled * jnp.mean(grad_scaled * scaled, axis=-1, keepdims=True))
    return grad_values, grad_gain


def rotary(heads32, rope_cos, rope_sin, sin_sign):
    half_dim = rope_cos.shape[-1]
    first_half = heads32[..., :half_dim]
    second_half = heads32[..., half_dim:]
    cos_b = rope_cos[None, :, None, :]
    sin_b = sin_sign * rope_sin[None, :, None, :]
    return jnp.concatenate([first_half * cos_b - second_half * sin_b, second_half * cos_b + first_half * sin_b], axis=-1)


def layer_forward(weights, rope_cos, rope_sin, hidden):
    w_query, w_key, w_value, w_out, w_gate, w_up, w_down, gain_attn, gain_mlp = weights
    batch_size = hidden.shape[0]
    seq_len = hidden.shape[1]
    head_dim = 2 * rope_cos.shape[-1]
    kv_heads = w_key.shape[1] // head_dim
    num_heads = w_query.shape[1] // head_dim
    group_size = num_heads // kv_heads
    normed, inv_rms_attn = rms_forward(hidden, gain_attn)
    q_proj = jnp.einsum("bsd,df->bsf", normed, w_query, preferred_element_type=jnp.float32)
    q_heads = rotary(q_proj.reshape(batch_size, seq_len, num_heads, head_dim), rope_cos, rope_sin, 1.0)
    q_heads = q_heads.astype(jnp.bfloat16).reshape(batch_size, seq_len, kv_heads, group_size, head_dim)
    k_proj = jnp.einsum("bsd,df->bsf", normed, w_key, preferred_element_type=jnp.float32)
    k_heads = rotary(k_proj.reshape(batch_size, seq_len, kv_heads, head_dim), rope_cos, rope_sin, 1.0).astype(jnp.bfloat16)
    v_heads = jnp.einsum("bsd,df->bsf", normed, w_value, preferred_element_type=jnp.float32)
    v_heads = v_heads.astype(jnp.bfloat16).reshape(batch_size, seq_len, kv_heads, head_dim)
    scores = jnp.einsum("bqkgd,bskd->bkgqs", q_heads, k_heads, preferred_element_type=jnp.float32) * head_dim ** -0.5
    positions = jnp.arange(seq_len)
    scores = jnp.where(positions[:, None] >= positions[None, :], scores, MASK_VALUE)
    attn_probs = jax.nn.softmax(scores, axis=-1).astype(jnp.bfloat16)
    attn_heads = jnp.einsum("bkgqs,bskd->bqkgd", attn_probs, v_heads, preferred_element_type=jnp.float32)
    attn_heads = attn_heads.astype(jnp.bfloat16).reshape(batch_size, seq_len, num_heads * head_dim)
    attn_proj = jnp.einsum("bsf,fd->bsd", attn_heads, w_out, preferred_element_type=jnp.float32)
    mid_hidden = (hidden.astype(jnp.float32) + attn_proj).astype(jnp.bfloat16)
    normed_mlp, inv_rms_mlp = rms_forward(mid_hidden, gain_mlp)
    gate_pre = jnp.einsum("bsd,df->bsf", normed_mlp, w_gate, preferred_element_type=jnp.float32)
    up_proj = jnp.einsum("bsd,df->bsf", normed_mlp, w_up, preferred_element_type=jnp.float32)
    mlp_act = (jax.nn.silu(gate_pre) * up_proj).astype(jnp.bfloat16)
    down_proj = jnp.einsum("bsf,fd->bsd", mlp_act, w_down, preferred_element_type=jnp.float32)
    out_hidden = (mid_hidden.astype(jnp.float32) + down_proj).astype(jnp.bfloat16)
    saved_acts = (hidden, inv_rms_attn, normed, q_heads, k_heads, v_heads, attn_probs, attn_heads, mid_hidden, inv_rms_mlp, normed_mlp, gate_pre, up_proj, mlp_act)
    return out_hidden, saved_acts


def layer_backward(weights, rope_cos, rope_sin, saved_acts, grad_out):
    w_query, w_key, w_value, w_out, w_gate, w_up, w_down, gain_attn, gain_mlp = weights
    (hidden, inv_rms_attn, normed, q_heads, k_heads, v_heads, attn_probs, attn_heads, mid_hidden, inv_rms_mlp, normed_mlp, gate_pre, up_proj, mlp_act) = saved_acts
    batch_size = hidden.shape[0]
    seq_len = hidden.shape[1]
    head_dim = 2 * rope_cos.shape[-1]
    kv_heads = k_heads.shape[2]
    num_heads = kv_heads * q_heads.shape[3]
    grad_w_down = jnp.einsum("bsf,bsd->fd", mlp_act, grad_out, preferred_element_type=jnp.float32)
    grad_act = jnp.einsum("bsd,fd->bsf", grad_out, w_down, preferred_element_type=jnp.float32)
    gate_sig = jax.nn.sigmoid(gate_pre)
    grad_up = (grad_act * gate_pre * gate_sig).astype(jnp.bfloat16)
    grad_gate = (grad_act * up_proj * gate_sig * (1.0 + gate_pre * (1.0 - gate_sig))).astype(jnp.bfloat16)
    grad_w_gate = jnp.einsum("bsd,bsf->df", normed_mlp, grad_gate, preferred_element_type=jnp.float32)
    grad_w_up = jnp.einsum("bsd,bsf->df", normed_mlp, grad_up, preferred_element_type=jnp.float32)
    grad_normed_mlp = (jnp.einsum("bsf,df->bsd", grad_gate, w_gate, preferred_element_type=jnp.float32)
                       + jnp.einsum("bsf,df->bsd", grad_up, w_up, preferred_element_type=jnp.float32))
    grad_mid_norm, grad_gain_mlp = rms_backward(mid_hidden, inv_rms_mlp, gain_mlp, grad_normed_mlp)
    grad_mid = grad_out.astype(jnp.float32) + grad_mid_norm
    grad_mid_bf = grad_mid.astype(jnp.bfloat16)
    grad_w_out = jnp.einsum("bsf,bsd->fd", attn_heads, grad_mid_bf, preferred_element_type=jnp.float32)
    grad_attn = jnp.einsum("bsd,fd->bsf", grad_mid_bf, w_out, preferred_element_type=jnp.float32)
    grad_attn = grad_attn.astype(jnp.bfloat16).reshape(batch_size, seq_len, kv_heads, -1, head_dim)
    grad_v = jnp.einsum("bkgqs,bqkgd->bskd", attn_probs, grad_attn, preferred_element_type=jnp.float32)
    grad_v = grad_v.astype(jnp.bfloat16).reshape(batch_size, seq_len, -1)
    grad_probs = jnp.einsum("bqkgd,bskd->bkgqs", grad_attn, v_heads, preferred_element_type=jnp.float32)
    probs32 = attn_probs.astype(jnp.float32)
    grad_scores = probs32 * (grad_probs - jnp.sum(probs32 * grad_probs, axis=-1, keepdims=True)) * head_dim ** -0.5
    grad_scores = grad_scores.astype(jnp.bfloat16)
    grad_q = jnp.einsum("bkgqs,bskd->bqkgd", grad_scores, k_heads, preferred_element_type=jnp.float32)
    grad_q = rotary(grad_q.reshape(batch_size, seq_len, num_heads, head_dim), rope_cos, rope_sin, -1.0)
    grad_q = grad_q.astype(jnp.bfloat16).reshape(batch_size, seq_len, -1)
    grad_k = jnp.einsum("bkgqs,bqkgd->bskd", grad_scores, q_heads, preferred_element_type=jnp.float32)
    grad_k = rotary(grad_k, rope_cos, rope_sin, -1.0).astype(jnp.bfloat16).reshape(batch_size, seq_len, -1)
    grad_w_query = jnp.einsum("bsd,bsf->df", normed, grad_q, preferred_element_type=jnp.float32)
    grad_w_key = jnp.einsum("bsd,bsf->df", normed, grad_k, preferred_element_type=jnp.float32)
    grad_w_value = jnp.einsum("bsd,bsf->df", normed, grad_v, preferred_element_type=jnp.float32)
    grad_normed = (jnp.einsum("bsf,df->bsd", grad_q, w_query, preferred_element_type=jnp.float32)
                   + jnp.einsum("bsf,df->bsd", grad_k, w_key, preferred_element_type=jnp.float32)
                   + jnp.einsum("bsf,df->bsd", grad_v, w_value, preferred_element_type=jnp.float32))
    grad_hidden_norm, grad_gain_attn = rms_backward(hidden, inv_rms_attn, gain_attn, grad_normed)
    grad_hidden = (grad_mid + grad_hidden_norm).astype(jnp.bfloat16)
    layer_grads = (grad_w_query, grad_w_key, grad_w_value, grad_w_out, grad_w_gate, grad_w_up, grad_w_down, grad_gain_attn, grad_gain_mlp)
    return grad_hidden, layer_grads


def solution(mesh):
    shard_spec = P(None, "fsdp")
    batch_spec = P("fsdp")

    def gather_layer(masters, layer_idx):
        return tuple(lax.all_gather(master[layer_idx].astype(jnp.bfloat16), "fsdp", axis=0, tiled=True) for master in masters)

    def local_step(w_query, w_key, w_value, w_out, w_gate, w_up, w_down, gain_attn, gain_mlp, rope_cos, rope_sin, x_in, y_cot):
        masters = (w_query, w_key, w_value, w_out, w_gate, w_up, w_down, gain_attn, gain_mlp)
        num_layers = w_query.shape[0]
        hidden = x_in
        saved_layers = []
        for layer_idx in range(num_layers):
            weights = gather_layer(masters, layer_idx)
            hidden, saved_acts = layer_forward(weights, rope_cos, rope_sin, hidden)
            saved_layers.append(saved_acts)
        masters, saved_layers, hidden = lax.optimization_barrier((masters, saved_layers, hidden))
        grad_hidden = y_cot
        grad_layers = []
        for layer_idx in reversed(range(num_layers)):
            weights = gather_layer(masters, layer_idx)
            grad_hidden, layer_grads = layer_backward(weights, rope_cos, rope_sin, saved_layers[layer_idx], grad_hidden)
            grad_layers.insert(0, tuple(lax.psum_scatter(grad_full, "fsdp", scatter_dimension=0, tiled=True) for grad_full in layer_grads))
        grad_stacked = tuple(jnp.stack([layer_part[tensor_idx] for layer_part in grad_layers]) for tensor_idx in range(len(masters)))
        return (hidden, grad_hidden) + grad_stacked

    in_specs = (shard_spec,) * 9 + (P(), P(), batch_spec, batch_spec)
    out_specs = (batch_spec, batch_spec) + (shard_spec,) * 9
    return jax.shard_map(local_step, mesh=mesh, in_specs=in_specs, out_specs=out_specs, check_vma=False)
```

profile of v0, /device:TPU:0, one launch (start us, length us, event | category | flops | bytes accessed | tf_op | source)
XLA Modules:
  0.0 2758.2 jit_solution(17369471318178681594)
XLA Ops:
  23.8 35.4 %all-reduce.38 = (bf16[960]{0:T(1024)(128)(2,1)S(1)}, bf16[960]{0:T(1024)(128)(2,1)S(1)}, bf16[960]{0:T(1024)(128)(2,1)S(1)}, bf16[960]{0:T(1024)(128)(2,1)S(1)}) all-reduce(bf16[960]{0:T(1024)(128)(2,1)S(1)} %dynamic-update-slice, bf16[960]{0:T(1024)(128)(2,1)S(1)} %dynamic-update-slice.1, ...), channel_id=2, replica_groups=mesh['fsdp'=16] {'fsdp'}, use_global_device_ids=true, to_apply=%add | all-reduce | flops 3840 | bytes 15360
  214.1 29.5 %fusion.181 = (f32[16,5,3,256]{3,2,1,0:T(4,128)S(1)}, f32[16,5,3,256,256]{3,4,2,1,0:T(8,128)}) fusion(pred[256,256]{0,1:T(8,128)(4,1)S(1)} %iota_compare_fusion, bf16[16,256,5,32]{1,3,2,0:T(8,128)(2,1)} %copy-done.28, bf16[16,256,5,32]{1,3,2,0:T(8,128)(2,1)} %copy-done.27, bf16[16,256,5,3,32]{1,4,3,2,0:T(8,128)(2,1)} %bitcast.494, ...), kind=kOutput, calls=%fused_computation.292 | convolution fusion | flops 2097152256 | bytes 73711616 | tf_op jit(solution)/shard_map/sub | solution.py:53
  243.6 32.6 %divide_convert_fusion.1 = bf16[16,5,3,256,256]{3,4,2,1,0:T(8,128)(2,1)} fusion(f32[16,5,3,256,256]{3,4,2,1,0:T(8,128)} %get-tuple-element.229, f32[16,5,3,256]{3,2,1,0:T(4,128)S(1)} %get-tuple-element.228), kind=kLoop, calls=%fused_computation.18 | loop fusion | flops 31457280 | bytes 94617600 | tf_op jit(solution)/shard_map/convert_element_type | solution.py:53
  346.6 31.1 %fusion.84 = f32[16,256,2560]{2,1,0:T(8,128)} fusion(bf16[16,256,960]{1,2,0:T(8,128)(2,1)} %fusion.45, bf16[1,960,2560]{2,0,1:T(2,128)(2,1)} %all-gather.61.cloned.1.call-done), kind=kOutput, calls=%fused_computation.146 | convolution fusion | flops 20132659200 | bytes 54722560 | tf_op jit(solution)/shard_map/bsd,df->bsf/dot_general | solution.py:59
  377.8 52.1 %multiply_convert_fusion.3 = (bf16[16,256,2560]{2,1,0:T(8,128)(2,1)}, f32[16,256,2560]{2,1,0:T(8,128)}) fusion(f32[16,256,2560]{2,1,0:T(8,128)} %fusion.84, bf16[16,256,960]{1,2,0:T(8,128)(2,1)} %fusion.45, bf16[1,960,2560]{2,0,1:T(2,128)(2,1)} %all-gather.63.cloned.1.call-done), kind=kOutput, calls=%fused_computation.36 | convolution fusion | flops 20195573760 | bytes 117637120 | tf_op jit(solution)/shard_map/bsd,df->bsf/dot_general | solution.py:60
  429.9 27.2 fusion.47
  488.6 29.8 %fusion.186 = (f32[16,5,3,256]{3,2,1,0:T(4,128)S(1)}, f32[16,5,3,256,256]{3,4,2,1,0:T(8,128)}) fusion(pred[256,256]{0,1:T(8,128)(4,1)S(1)} %copy-done.64, bf16[16,256,5,32]{1,3,2,0:T(8,128)(2,1)} %get-tuple-element.181, bf16[16,256,5,32]{1,3,2,0:T(8,128)(2,1)} %get-tuple-element.180, bf16[16,256,5,3,32]{1,4,3,2,0:T(8,128)(2,1)} %bitcast.489, ...), kind=kOutput, calls=%fused_computation.293 | convolution fusion | flops 2097152256 | bytes 73711616 | tf_op jit(solution)/shard_map/sub | solution.py:53
  518.4 31.6 %divide_convert_fusion = bf16[16,5,3,256,256]{3,4,2,1,0:T(8,128)(2,1)} fusion(f32[16,5,3,256,256]{3,4,2,1,0:T(8,128)} %get-tuple-element.237, f32[16,5,3,256]{3,2,1,0:T(4,128)S(1)} %get-tuple-element.236), kind=kLoop, calls=%fused_computation.16 | loop fusion | flops 31457280 | bytes 94617600 | tf_op jit(solution)/shard_map/convert_element_type | solution.py:53
  587.7 31.2 %fusion.78 = f32[16,256,2560]{2,1,0:T(8,128)} fusion(bf16[16,256,960]{1,2,0:T(8,128)(2,1)} %fusion.53, bf16[1,960,2560]{2,0,1:T(2,128)(2,1)} %all-gather.71.cloned.1.call-done), kind=kOutput, calls=%fused_computation.140 | convolution fusion | flops 20132659200 | bytes 54722560 | tf_op jit(solution)/shard_map/bsd,df->bsf/dot_general | solution.py:59
  628.4 51.2 %multiply_convert_fusion.2 = (bf16[16,256,2560]{2,1,0:T(8,128)(2,1)}, f32[16,256,2560]{2,1,0:T(8,128)}) fusion(f32[16,256,2560]{2,1,0:T(8,128)} %fusion.78, bf16[16,256,960]{1,2,0:T(8,128)(2,1)} %fusion.53, bf16[1,960,2560]{2,0,1:T(2,128)(2,1)} %all-gather.73.cloned.1.call-done), kind=kOutput, calls=%fused_computation.35 | convolution fusion | flops 20195573760 | bytes 117637120 | tf_op jit(solution)/shard_map/bsd,df->bsf/dot_general | solution.py:60
  679.6 27.4 fusion.54
  720.1 32.8 %all-reduce.37 = (bf16[960]{0:T(1024)(128)(2,1)S(1)}, bf16[960]{0:T(1024)(128)(2,1)S(1)}, bf16[960]{0:T(1024)(128)(2,1)S(1)}, bf16[960]{0:T(1024)(128)(2,1)S(1)}) all-reduce(bf16[960]{0:T(1024)(128)(2,1)S(1)} %dynamic-update-slice.4, bf16[960]{0:T(1024)(128)(2,1)S(1)} %dynamic-update-slice.5, ...), channel_id=23, replica_groups=mesh['fsdp'=16] {'fsdp'}, use_global_device_ids=true, to_apply=%add.4 | all-reduce | flops 3840 | bytes 15360
  838.2 28.9 %convolution_bitcast_fusion = f32[2560,960]{1,0:T(8,128)} fusion(bf16[16,256,2560]{2,1,0:T(8,128)(2,1)} %get-tuple-element.86, bf16[16,256,960]{1,2,0:T(8,128)(2,1)} %param.25), kind=kOutput, calls=%fused_computation.113 | convolution fusion | flops 20132659200 | bytes 38666240 | tf_op jit(solution)/shard_map/bsf,bsd->fd/dot_general | solution.py:76
  867.4 55.2 %fusion.28 = (bf16[16,256,2560]{2,1,0:T(8,128)(2,1)}, bf16[16,256,2560]{2,1,0:T(8,128)(2,1)}) fusion(f32[16,256,2560]{2,1,0:T(8,128)} %fusion.78, f32[16,256,2560]{2,1,0:T(8,128)} %get-tuple-element.52, bf16[16,256,960]{1,2,0:T(8,128)(2,1)} %param.25, bf16[1,2560,960]{2,1,0:T(8,128)(2,1)} %all-gather.77.cloned.1.call-done), kind=kOutput, calls=%fused_computation.30 | convolution fusion | flops 20268974080 | bytes 138608640 | tf_op jit(solution)/shard_map/bsd,fd->bsf/dot_general | solution.py:77
  922.6 28.5 %fusion.72 = f32[16,256,960]{1,2,0:T(8,128)} fusion(bf16[16,256,2560]{2,1,0:T(8,128)(2,1)} %get-tuple-element.167, bf16[1,960,2560]{2,0,1:T(2,128)(2,1)} %all-gather.79.cloned.1.call-done), kind=kOutput, calls=%fused_computation.134 | convolution fusion | flops 20132659200 | bytes 41615360 | tf_op jit(solution)/shard_map/bsf,df->bsd/dot_general | solution.py:83
  951.1 33.5 %multiply_reduce_fusion = (f32[960]{0:T(1024)}, f32[16,256]{1,0:T(8,128)S(1)}, f32[16,256,960]{1,2,0:T(8,128)}) fusion(bf16[16,256,960]{1,2,0:T(8,128)(2,1)} %copy-done.2, f32[16,256]{1,0:T(8,128)S(1)} %bitcast.521, f32[960]{0:T(1024)S(1)} %copy-done.70, f32[16,256,960]{1,2,0:T(8,128)} %fusion.72, bf16[16,256,2560]{2,1,0:T(8,128)(2,1)} %get-tuple-element.166, ...), kind=kOutput, calls=%fused_computation.75 | convolution fusion | flops 20164112384 | bytes 65248768 | tf_op jit(solution)/shard_map/bsf,df->bsd/dot_general | solution.py:84
  1016.3 27.0 fusion.96
  1060.6 67.7 %fusion.32 = f32[16,5,64,3,256]{4,2,3,1,0:T(8,128)} fusion(bf16[16,5,3,256,256]{3,4,2,1,0:T(8,128)(2,1)} %divide_convert_fusion, f32[16,5,256,256,3]{3,2,4,1,0:T(8,128)} %fusion.96, bf16[16,256,5,64]{1,3,2,0:T(8,128)(2,1)} %pad_maximum_fusion.5), kind=kOutput, calls=%fused_computation.40 | convolution fusion | flops 2123428096 | bytes 112721920 | tf_op jit(solution)/shard_map/bkgqs,bskd->bqkgd/dot_general | solution.py:97
  1128.2 64.4 %fusion.113 = f32[16,256,5,64]{1,3,2,0:T(8,128)} fusion(bf16[16,256,5,3,64]{1,4,3,2,0:T(8,128)(2,1)} %pad_maximum_fusion.1, bf16[16,5,3,256,256]{3,4,2,1,0:T(8,128)(2,1)} %divide_convert_fusion, f32[16,5,256,256,3]{3,2,4,1,0:T(8,128)} %fusion.96), kind=kOutput, calls=%fused_computation.179 | convolution fusion | flops 2123428096 | bytes 107479040 | tf_op jit(solution)/shard_map/bkgqs,bqkgd->bskd/dot_general | solution.py:100
  1231.0 26.2 multiply_reduce_fusion.2
  1269.9 54.8 %multiply_convert_fusion = (bf16[16,256,2560]{2,1,0:T(8,128)(2,1)}, bf16[16,256,2560]{2,1,0:T(8,128)(2,1)}) fusion(f32[16,256,2560]{2,1,0:T(8,128)} %fusion.84, f32[16,256,2560]{2,1,0:T(8,128)} %get-tuple-element.70, bf16[16,256,960]{1,2,0:T(8,128)(2,1)} %add_convert_fusion.1, bf16[1,2560,960]{2,1,0:T(8,128)(2,1)} %all-gather.87.cloned.1.call-done), kind=kOutput, calls=%fused_computation.31 | convolution fusion | flops 20268974080 | bytes 138608640 | tf_op jit(solution)/shard_map/bsd,fd->bsf/dot_general | solution.py:77
  1324.7 28.7 %fusion.67 = f32[16,256,960]{1,2,0:T(8,128)} fusion(bf16[16,256,2560]{2,1,0:T(8,128)(2,1)} %get-tuple-element.165, bf16[1,960,2560]{2,0,1:T(2,128)(2,1)} %all-gather.89.cloned.1.call-done), kind=kOutput, calls=%fused_computation.129 | convolution fusion | flops 20132659200 | bytes 41615360 | tf_op jit(solution)/shard_map/bsf,df->bsd/dot_general | solution.py:83
  1353.5 32.9 %multiply_reduce_fusion.1 = (f32[960]{0:T(1024)}, f32[16,256]{1,0:T(8,128)S(1)}, f32[16,256,960]{1,2,0:T(8,128)}) fusion(bf16[16,256,960]{1,2,0:T(8,128)(2,1)} %copy-done, f32[16,256]{1,0:T(8,128)S(1)} %bitcast.517, f32[960]{0:T(1024)S(1)} %copy-done.68, f32[16,256,960]{1,2,0:T(8,128)} %fusion.67, bf16[16,256,2560]{2,1,0:T(8,128)(2,1)} %get-tuple-element.164, ...), kind=kOutput, calls=%fused_computation.76 | convolution fusion | flops 20164112384 | bytes 65248768 | tf_op jit(solution)/shard_map/bsf,df->bsd/dot_general | solution.py:84
  1442.8 64.0 %fusion.30 = f32[16,5,64,3,256]{4,2,3,1,0:T(8,128)} fusion(bf16[16,5,3,256,256]{3,4,2,1,0:T(8,128)(2,1)} %divide_convert_fusion.1, f32[16,5,256,256,3]{3,2,4,1,0:T(8,128)} %fusion.93, bf16[16,256,5,64]{1,3,2,0:T(8,128)(2,1)} %pad_maximum_fusion.4), kind=kOutput, calls=%fused_computation.38 | convolution fusion | flops 2123428096 | bytes 112721920 | tf_op jit(solution)/shard_map/bkgqs,bskd->bqkgd/dot_general | solution.py:97
  1515.8 62.4 %fusion.114 = f32[16,256,5,64]{1,3,2,0:T(8,128)} fusion(bf16[16,256,5,3,64]{1,4,3,2,0:T(8,128)(2,1)} %pad_maximum_fusion, bf16[16,5,3,256,256]{3,4,2,1,0:T(8,128)(2,1)} %divide_convert_fusion.1, f32[16,5,256,256,3]{3,2,4,1,0:T(8,128)} %fusion.93), kind=kOutput, calls=%fused_computation.180 | convolution fusion | flops 2123428096 | bytes 107479040 | tf_op jit(solution)/shard_map/bkgqs,bqkgd->bskd/dot_general | solution.py:100
  1583.3 31.7 %convolution_bitcast_fusion.3 = f32[960,2560]{1,0:T(8,128)} fusion(bf16[16,256,960]{1,2,0:T(8,128)(2,1)} %fusion.45, bf16[16,256,2560]{2,1,0:T(8,128)(2,1)} %get-tuple-element.164), kind=kOutput, calls=%fused_computation.116 | convolution fusion | flops 20132659200 | bytes 38666240 | tf_op jit(solution)/shard_map/bsd,bsf->df/dot_general | solution.py:82
  1637.9 217.5 %fusion.166 = (f32[64,2560]{1,0:T(8,128)S(1)}, f32[64,2560]{1,0:T(8,128)}) fusion(f32[960,2560]{1,0:T(8,128)} %convolution_bitcast_fusion.2, f32[960,2560]{1,0:T(8,128)} %convolution_bitcast_fusion.3), kind=kCustom, calls=%all-reduce-scatter.13 | all-reduce-scatter fusion | flops 5242881 | bytes 20971520
  1956.0 28.8 %convolution_bitcast_fusion.1 = f32[2560,960]{1,0:T(8,128)} fusion(bf16[16,256,2560]{2,1,0:T(8,128)(2,1)} %get-tuple-element.85, bf16[16,256,960]{1,2,0:T(8,128)(2,1)} %add_convert_fusion.1), kind=kOutput, calls=%fused_computation.114 | convolution fusion | flops 20132659200 | bytes 38666240 | tf_op jit(solution)/shard_map/bsf,bsd->fd/dot_general | solution.py:76
  1984.8 31.5 %convolution_bitcast_fusion.5 = f32[960,2560]{1,0:T(8,128)} fusion(bf16[16,256,960]{1,2,0:T(8,128)(2,1)} %fusion.45, bf16[16,256,2560]{2,1,0:T(8,128)(2,1)} %get-tuple-element.165), kind=kOutput, calls=%fused_computation.118 | convolution fusion | flops 20132659200 | bytes 38666240 | tf_op jit(solution)/shard_map/bsd,bsf->df/dot_general | solution.py:81
  2041.6 29.1 %convolution_bitcast_fusion.4 = f32[960,2560]{1,0:T(8,128)} fusion(bf16[16,256,960]{1,2,0:T(8,128)(2,1)S(1)} %bitcast.506, bf16[16,256,2560]{2,1,0:T(8,128)(2,1)} %get-tuple-element.167), kind=kOutput, calls=%fused_computation.117 | convolution fusion | flops 20132659200 | bytes 38666240 | tf_op jit(solution)/shard_map/bsd,bsf->df/dot_general | solution.py:81
  2070.7 503.1 %fusion.165 = (f32[64,960]{1,0:T(8,128)S(1)}, f32[64,960]{1,0:T(8,128)}, f32[64,320]{1,0:T(8,128)}, f32[64,320]{1,0:T(8,128)}, f32[64,320]{1,0:T(8,128)}, /*inde...) fusion(f32[960,960]{1,0:T(8,128)} %convolution_bitcast_fusion.6, ...), kind=kCustom, calls=%all-reduce-scatter.12 | all-reduce-scatter fusion | flops 10485761 | bytes 41943040
  2635.7 32.2 %all-reduce.36 = (f32[960]{0:T(1024)S(1)}, f32[960]{0:T(1024)S(1)}, f32[960]{0:T(1024)S(1)}, f32[960]{0:T(1024)S(1)}) all-reduce(f32[960]{0:T(1024)S(1)} %copy-done.72, f32[960]{0:T(1024)S(1)} %get-tuple-element.124, f32[960]{0:T(1024)S(1)} %copy-done.71, f32[960]{0:T(1024)S(1)} %copy-done.73), channel_id=53, replica_groups=mesh['fsdp'=16] {'fsdp'}, use_global_device_ids=true, to_apply=%region_31.32.clone | all-reduce | flops 3840 | bytes 30720
  (482 shorter events, 882.3 us)
Async XLA Ops:
  7.2 172.2 %all-gather.57.cloned.1.call-start = ((), (), s32[]{:S(2)}) async-start(), calls=%async_computation.4 | async-start | bytes 4177920 | tf_op jit(solution)/shard_map/all_gather | solution.py:119
  9.8 283.2 %all-gather.59.cloned.1.call-start = ((), (), s32[]{:S(2)}) async-start(), calls=%async_computation.5 | async-start | bytes 4177920 | tf_op jit(solution)/shard_map/all_gather | solution.py:119
  12.2 313.3 %all-gather.67.cloned.1.call-start = ((), (), s32[]{:S(2)}) async-start(), calls=%async_computation.9 | async-start | bytes 4177920 | tf_op jit(solution)/shard_map/all_gather | solution.py:119
  12.9 323.1 %all-gather.69.cloned.1.call-start = ((), (), s32[]{:S(2)}) async-start(), calls=%async_computation.10 | async-start | bytes 4177920 | tf_op jit(solution)/shard_map/all_gather | solution.py:119
  13.5 333.1 %all-gather.61.cloned.1.call-start = ((), (), s32[]{:S(2)}) async-start(), calls=%async_computation.6 | async-start | bytes 10444800 | tf_op jit(solution)/shard_map/all_gather | solution.py:119
  17.2 360.6 %all-gather.63.cloned.1.call-start = ((), (), s32[]{:S(2)}) async-start(), calls=%async_computation.7 | async-start | bytes 10444800 | tf_op jit(solution)/shard_map/all_gather | solution.py:119
  19.6 410.3 %all-gather.65.cloned.1.call-start = ((), (), s32[]{:S(2)}) async-start(), calls=%async_computation.8 | async-start | bytes 5570560 | tf_op jit(solution)/shard_map/all_gather | solution.py:119
  20.7 567.0 %all-gather.71.cloned.1.call-start = ((), (), s32[]{:S(2)}) async-start(), calls=%async_computation.11 | async-start | bytes 10444800 | tf_op jit(solution)/shard_map/all_gather | solution.py:119
  21.4 607.0 %all-gather.73.cloned.1.call-start = ((), (), s32[]{:S(2)}) async-start(), calls=%async_computation.12 | async-start | bytes 10444800 | tf_op jit(solution)/shard_map/all_gather | solution.py:119
  22.2 657.4 %all-gather.75.cloned.1.call-start = ((), (), s32[]{:S(2)}) async-start(), calls=%async_computation.13 | async-start | bytes 5570560 | tf_op jit(solution)/shard_map/all_gather | solution.py:119
  22.7 844.7 %all-gather.77.cloned.1.call-start = ((), (), s32[]{:S(2)}) async-start(), calls=%async_computation.14 | async-start | bytes 5570560 | tf_op jit(solution)/shard_map/all_gather | solution.py:119
  708.1 214.6 %all-gather.79.cloned.1.call-start = ((), (), s32[]{:S(2)}) async-start(), calls=%async_computation.15 | async-start | bytes 10444800 | tf_op jit(solution)/shard_map/all_gather | solution.py:119
  710.9 240.2 %all-gather.81.cloned.1.call-start = ((), (), s32[]{:S(2)}) async-start(), calls=%async_computation.16 | async-start | bytes 10444800 | tf_op jit(solution)/shard_map/all_gather | solution.py:119
  713.3 287.6 %all-gather.83.cloned.1.call-start = ((), (), s32[]{:S(2)}) async-start(), calls=%async_computation.17 | async-start | bytes 4177920 | tf_op jit(solution)/shard_map/all_gather | solution.py:119
  714.7 516.3 %all-gather.85.cloned.1.call-start = ((), (), s32[]{:S(2)}) async-start(), calls=%async_computation.18 | async-start | bytes 4177920 | tf_op jit(solution)/shard_map/all_gather | solution.py:119
  716.0 553.8 %all-gather.87.cloned.1.call-start = ((), (), s32[]{:S(2)}) async-start(), calls=%async_computation.19 | async-start | bytes 5570560 | tf_op jit(solution)/shard_map/all_gather | solution.py:119
  716.6 608.1 %all-gather.89.cloned.1.call-start = ((), (), s32[]{:S(2)}) async-start(), calls=%async_computation.20 | async-start | bytes 10444800 | tf_op jit(solution)/shard_map/all_gather | solution.py:119
  717.2 636.3 %all-gather.91.cloned.1.call-start = ((), (), s32[]{:S(2)}) async-start(), calls=%async_computation.21 | async-start | bytes 10444800 | tf_op jit(solution)/shard_map/all_gather | solution.py:119
  717.8 684.7 %all-gather.93.cloned.1.call-start = ((), (), s32[]{:S(2)}) async-start(), calls=%async_computation.22 | async-start | bytes 4177920 | tf_op jit(solution)/shard_map/all_gather | solution.py:119
  718.5 1892.8 %all-gather.95.cloned.1.call-start = ((), (), s32[]{:S(2)}) async-start(), calls=%async_computation.23 | async-start | bytes 4177920 | tf_op jit(solution)/shard_map/all_gather | solution.py:119
  838.2 1910.5 %reduce-scatter.29.cloned.1.call-start = ((), (), s32[]{:S(2)}) async-start(), calls=%async_computation.3 | async-start | bytes 11141120 | tf_op jit(solution)/shard_map/reduce_scatter | solution.py:136
  867.1 1881.5 %reduce-scatter.27.cloned.1.call-start = ((), (), s32[]{:S(2)}) async-start(), calls=%async_computation.2 | async-start | bytes 11141120 | tf_op jit(solution)/shard_map/reduce_scatter | solution.py:136
  1857.6 867.8 %collective-permute-start.10 = (f32[60,2560]{1,0:T(8,128)}, f32[60,2560]{1,0:T(8,128)}, u32[]{:S(2)}, u32[]{:S(2)}) collective-permute-start(f32[60,2560]{1,0:T(8,128)} %slice.298), channel_id=1, source_target_pairs={{0,1},{1,2},{2,3},{3,4},{4,5},{5,6},{6,7},{7,8},{8,9},{9,10},{10,1... | collective-permute-start | bytes 1843208
  1860.6 870.6 %collective-permute-start.11 = (f32[60,2560]{1,0:T(8,128)}, f32[60,2560]{1,0:T(8,128)}, u32[]{:S(2)}, u32[]{:S(2)}) collective-permute-start(f32[60,2560]{1,0:T(8,128)} %slice.299), channel_id=1, source_target_pairs={{0,1},{1,2},{2,3},{3,4},{4,5},{5,6},{6,7},{7,8},{8,9},{9,10},{10,1... | collective-permute-start | bytes 1843208
  2575.8 165.5 %collective-permute-start.8 = (f32[60,2560]{1,0:T(8,128)}, f32[60,2560]{1,0:T(8,128)}, u32[]{:S(2)}, u32[]{:S(2)}) collective-permute-start(f32[60,2560]{1,0:T(8,128)} %slice.296), channel_id=1, source_target_pairs={{0,1},{1,2},{2,3},{3,4},{4,5},{5,6},{6,7},{7,8},{8,9},{9,10},{10,1... | collective-permute-start | bytes 1843208
  2583.7 102.8 %collective-permute-start.4 = (f32[60,320]{1,0:T(8,128)}, f32[60,320]{1,0:T(8,128)}, u32[]{:S(2)}, u32[]{:S(2)}) collective-permute-start(f32[60,320]{1,0:T(8,128)} %slice.292), channel_id=1, source_target_pairs={{0,1},{1,2},{2,3},{3,4},{4,5},{5,6},{6,7},{7,8},{8,9},{9,10},{10,1... | collective-permute-start | bytes 230408
  2587.2 102.4 %collective-permute-start.5 = (f32[60,320]{1,0:T(8,128)}, f32[60,320]{1,0:T(8,128)}, u32[]{:S(2)}, u32[]{:S(2)}) collective-permute-start(f32[60,320]{1,0:T(8,128)} %slice.293), channel_id=1, source_target_pairs={{0,1},{1,2},{2,3},{3,4},{4,5},{5,6},{6,7},{7,8},{8,9},{9,10},{10,1... | collective-permute-start | bytes 230408
  2696.6 11.5 collective-permute-start.6
  2699.7 12.3 collective-permute-start.7
  2708.1 11.4 collective-permute-start
  2712.0 10.8 collective-permute-start.1
  2719.5 24.4 collective-permute-start.9
  (97 other events, 2803.5 us)
Sparse Core Ops, SparseCore 0:
  10.2 37.9 all-gather.56
  50.4 37.5 all-gather.58
  90.2 34.6 all-gather.66
  127.0 37.8 all-gather.68
  166.9 53.8 all-gather.60
  222.9 53.6 all-gather.62
  279.4 38.7 all-gather.64
  320.4 53.6 all-gather.70
  376.4 53.6 all-gather.72
  432.7 38.7 all-gather.74
  708.1 39.8 all-gather.76
  750.7 60.8 all-gather.78
  813.8 54.5 all-gather.80
  870.4 34.4 all-gather.82
  907.0 34.4 all-gather.84
  944.1 38.7 all-gather.86
  985.0 53.6 all-gather.88
  1040.8 53.6 all-gather.90
  1096.7 34.4 all-gather.92
  1133.3 34.4 all-gather.94
  1170.0 114.0 reduce-scatter.28
  2016.5 165.9 reduce-scatter.26
where the time goes:
time: 2770 us; the launch traced here: 2760 us
  matrix products  1330 us (48%)
  blocking collectives  958 us (35%)
  other arithmetic  253 us (9%)
  local copies, waits for them, and re-layouts  159 us (6%)
  starting transfers between devices  33.9 us (1%)
    unnamed x5, blocking collectives  821 us
    all_gather x8, blocking collectives, gather_layer(): lax.all_gather(master[layer_idx].astype(jnp.bfloat16), 'fsdp', axis=0, ti...  137 us
    dot_general x2, matrix products, layer_backward(): jnp.einsum('bkgqs,bskd->bqkgd', grad_scores, k_heads, preferred_element_t...  132 us
    dot_general x2, matrix products, layer_backward(): jnp.einsum('bkgqs,bqkgd->bskd', grad_scores, q_heads, preferred_element_t...  127 us
    dot_general x2, matrix products, layer_backward(): jnp.einsum('bsd,fd->bsf', grad_out, w_down, preferred_element_type=jnp.fl...  110 us
    dot_general x2, matrix products, layer_forward(): jnp.einsum('bsd,df->bsf', normed_mlp, w_up, preferred_element_type=jnp.fl...  103 us
    all_gather x12, local copies, waits for them, and re-layouts, gather_layer(): lax.all_gather(master[layer_idx].astype(jnp.bfloat16), 'fsdp', axis=0, ti...  72 us
    unnamed x240, local copies, waits for them, and re-layouts  68 us
  transfers between devices with their start and end apart: 34, of which 0 were waited for; matrix products, arithmetic and copies ran while one was open for 88% of the time, Pallas kernels for 0%

commit v1 on v0

v1 whole, which is shorter than its diff:
```python
import functools

import jax
import jax.numpy as jnp
from jax import lax
from jax.experimental import pallas as pl
from jax.experimental.pallas import tpu as pltpu
from jax.sharding import PartitionSpec as P


NORM_EPS = 1e-5
MASK_VALUE = -1e30
F32 = jnp.float32
BF16 = jnp.bfloat16

DEV = 16
D = 960
ROWS = D // DEV
PAD_ROWS = 64
FF = 2560
SHARD_FF = FF // DEV
KV = 320
HD = 64
KVH = 5
GROUP = 3
SEQ = 256
QKV = D + 2 * KV
AW = QKV + D
GAW = 2688
MW = 3 * FF
VMEM_LIMIT = 62 * 1024 * 1024
EXP_SCALE = HD ** -0.5 * 1.4426950408889634


def mm(a, b, ca=1, cb=0):
    return lax.dot_general(a, b, (((ca,), (cb,)), ((), ())), preferred_element_type=F32)


def params(**kw):
    return pltpu.CompilerParams(vmem_limit_bytes=VMEM_LIMIT, dimension_semantics=("arbitrary",), **kw)


def cost(flops, nbytes):
    return pl.CostEstimate(flops=int(flops), bytes_accessed=int(nbytes), transcendentals=0)


def const_spec(shape):
    zeros = (0,) * len(shape)
    return pl.BlockSpec(shape, lambda i: zeros, pipeline_mode=pl.Buffered(1))


ANY = pl.BlockSpec(memory_space=pl.ANY)


def inv_rms_of(vals32):
    return lax.rsqrt(jnp.mean(vals32 * vals32, axis=-1, keepdims=True) + NORM_EPS)


def unpack_shards(raw, buf, sems, place):
    def fetch(d):
        return pltpu.make_async_copy(raw.at[d], buf.at[d % 2], sems.at[d % 2])

    fetch(0).start()
    for d in range(DEV):
        if d + 1 < DEV:
            fetch(d + 1).start()
        fetch(d).wait()
        place(d, buf.at[d % 2])


def probs_t(k_t, q_t):
    scores = mm(k_t.T, q_t) * EXP_SCALE
    key = lax.broadcasted_iota(jnp.int32, scores.shape, 0)
    qry = lax.broadcasted_iota(jnp.int32, scores.shape, 1) & (SEQ - 1)
    scores = jnp.where(key <= qry, scores, MASK_VALUE)
    exps = jnp.exp2(scores - jnp.max(scores, axis=0, keepdims=True))
    return (exps * (1.0 / jnp.sum(exps, axis=0, keepdims=True))).astype(BF16)


def group_cols(ref, kv_head, seq):
    base = kv_head * GROUP * HD
    return jnp.concatenate([ref[base + g * HD: base + (g + 1) * HD, seq * SEQ:(seq + 1) * SEQ] for g in range(GROUP)], axis=1)


def attn_fwd_kernel(seqs, raw, x_ref, gain_ref, cos_ref, sin_ref, h_ref, qkv_ref, o_ref, wqkv_out, wo_out,
                    buf, wqkv_t, wo, sems, out_sems):
    step = pl.program_id(0)
    copies = (pltpu.make_async_copy(wqkv_t, wqkv_out, out_sems.at[0]), pltpu.make_async_copy(wo, wo_out, out_sems.at[1]))

    @pl.when(step == 0)
    def _():
        def place(d, shard):
            wo[d * ROWS:(d + 1) * ROWS, :] = shard[:ROWS, QKV:]
            rows = shard[:, :QKV].T
            wqkv_t[:, d * ROWS:(d + 1) * ROWS] = rows[:, :ROWS]

        unpack_shards(raw, buf, sems, place)
        for copy in copies:
            copy.start()

    x32 = x_ref[...].astype(F32)
    normed = (x32 * inv_rms_of(x32) * gain_ref[...]).astype(BF16)
    cos, sin = cos_ref[...], sin_ref[...]
    half = HD // 2
    for lo in range(0, QKV, KV):
        part = mm(wqkv_t[lo:lo + KV, :], normed, 1, 1)
        if lo < D + KV:
            for head in range(KV // HD):
                a = part[head * HD:head * HD + half]
                b = part[head * HD + half:(head + 1) * HD]
                qkv_ref[lo + head * HD:lo + head * HD + half, :] = (a * cos - b * sin).astype(BF16)
                qkv_ref[lo + head * HD + half:lo + (head + 1) * HD, :] = (b * cos + a * sin).astype(BF16)
        else:
            qkv_ref[lo:lo + KV, :] = part.astype(BF16)
    for seq in range(seqs):
        cols = slice(seq * SEQ, (seq + 1) * SEQ)
        for kvh in range(KVH):
            k_t = qkv_ref[D + kvh * HD:D + (kvh + 1) * HD, cols]
            v_t = qkv_ref[D + KV + kvh * HD:D + KV + (kvh + 1) * HD, cols]
            p_t = probs_t(k_t, group_cols(qkv_ref, kvh, seq))
            o_t = mm(v_t, p_t).astype(BF16)
            for g in range(GROUP):
                row = (kvh * GROUP + g) * HD
                o_ref[row:row + HD, cols] = o_t[:, g * SEQ:(g + 1) * SEQ]
    h_ref[...] = (x32 + mm(o_ref[...].T, wo[...])).astype(BF16)

    @pl.when(step == pl.num_programs(0) - 1)
    def _():
        for copy in copies:
            copy.wait()


def attn_fwd(raw, x, gain, cos_t, sin_t, seqs=2):
    tokens = x.shape[0]
    tm = seqs * SEQ
    row = pl.BlockSpec((tm, D), lambda i: (i, 0))
    col = lambda n: pl.BlockSpec((n, tm), lambda i: (0, i))
    return pl.pallas_call(
        functools.partial(attn_fwd_kernel, seqs),
        grid=(tokens // tm,),
        in_specs=[ANY, row, const_spec((1, D)), const_spec((HD // 2, tm)), const_spec((HD // 2, tm))],
        out_specs=[row, col(QKV), col(D), ANY, ANY],
        out_shape=[jax.ShapeDtypeStruct((tokens, D), BF16), jax.ShapeDtypeStruct((QKV, tokens), BF16),
                   jax.ShapeDtypeStruct((D, tokens), BF16), jax.ShapeDtypeStruct((QKV, D), BF16), jax.ShapeDtypeStruct((D, D), BF16)],
        scratch_shapes=[pltpu.VMEM((2, PAD_ROWS, AW), BF16), pltpu.VMEM((QKV, D), BF16), pltpu.VMEM((D, D), BF16),
                        pltpu.SemaphoreType.DMA((2,)), pltpu.SemaphoreType.DMA((2,))],
        compiler_params=params(), cost_estimate=cost(2 * tokens * D * AW * 1.6, tokens * 8000), name="attn_fwd",
    )(raw, x, gain, cos_t, sin_t)


def mlp_fwd_kernel(chunk, raw, h_ref, gain_ref, y_ref, g_ref, u_ref, n_ref, act_ref, wgu_out, wd_out,
                   buf, wgu, wd, sems, out_sems):
    step = pl.program_id(0)
    copies = (pltpu.make_async_copy(wgu, wgu_out, out_sems.at[0]), pltpu.make_async_copy(wd, wd_out, out_sems.at[1]))

    @pl.when(step == 0)
    def _():
        def place(d, shard):
            wgu[d * ROWS:(d + 1) * ROWS, :] = shard[:ROWS, :2 * FF]
            for i in range(10):
                for j in range(8):
                    unit = i * 8 + j
                    r, c = (unit // 20) * 16, 2 * FF + (unit % 20) * 128
                    width = min(128, D - j * 128)
                    wd[d * SHARD_FF + i * 16:d * SHARD_FF + (i + 1) * 16, j * 128:j * 128 + width] = shard[r:r + 16, c:c + width]

        unpack_shards(raw, buf, sems, place)
        for copy in copies:
            copy.start()

    h32 = h_ref[...].astype(F32)
    normed = (h32 * inv_rms_of(h32) * gain_ref[...]).astype(BF16)
    n_ref[...] = normed.T
    y_ref[...] = h_ref[...]
    out = h32
    for lo in range(0, FF, chunk):
        g = mm(normed, wgu[:, lo:lo + chunk])
        u = mm(normed, wgu[:, FF + lo:FF + lo + chunk])
        g_ref[:, lo:lo + chunk] = g
        u_ref[:, lo:lo + chunk] = u
        act = (g * (0.5 * jnp.tanh(0.5 * g) + 0.5) * u).astype(BF16)
        act_ref[lo:lo + chunk, :] = act.T
        out = out + mm(act, wd[lo:lo + chunk, :])
    y_ref[...] = out.astype(BF16)

    @pl.when(step == pl.num_programs(0) - 1)
    def _():
        for copy in copies:
            copy.wait()


def mlp_fwd(raw, h, gain, tm=256, chunk=1280):
    tokens = h.shape[0]
    row = lambda n: pl.BlockSpec((tm, n), lambda i: (i, 0))
    col = lambda n: pl.BlockSpec((n, tm), lambda i: (0, i))
    return pl.pallas_call(
        functools.partial(mlp_fwd_kernel, chunk),
        grid=(tokens // tm,),
        in_specs=[ANY, row(D), const_spec((1, D))],
        out_specs=[row(D), row(FF), row(FF), col(D), col(FF), ANY, ANY],
        out_shape=[jax.ShapeDtypeStruct((tokens, D), BF16), jax.ShapeDtypeStruct((tokens, FF), F32), jax.ShapeDtypeStruct((tokens, FF), F32),
                   jax.ShapeDtypeStruct((D, tokens), BF16), jax.ShapeDtypeStruct((FF, tokens), BF16),
                   jax.ShapeDtypeStruct((D, 2 * FF), BF16), jax.ShapeDtypeStruct((FF, D), BF16)],
        scratch_shapes=[pltpu.VMEM((2, PAD_ROWS, MW), BF16), pltpu.VMEM((D, 2 * FF), BF16), pltpu.VMEM((FF, D), BF16),
                        pltpu.SemaphoreType.DMA((2,)), pltpu.SemaphoreType.DMA((2,))],
        compiler_params=params(), cost_estimate=cost(2 * tokens * D * MW, tokens * 30000), name="mlp_fwd",
    )(raw, h, gain)


def mlp_bwd_kernel(chunk, dy_ref, h_ref, g_ref, u_ref, gain_ref, wgu, wd, dgu_ref, dmid_ref, dgain_ref):
    step = pl.program_id(0)
    dy = dy_ref[...]
    grad_normed = jnp.zeros((dy.shape[0], D), F32)
    for lo in range(0, FF, chunk):
        grad_act = mm(dy, wd[lo:lo + chunk, :], 1, 1)
        g = g_ref[:, lo:lo + chunk]
        u = u_ref[:, lo:lo + chunk]
        sig = 0.5 * jnp.tanh(0.5 * g) + 0.5
        grad_sig = grad_act * sig
        grad_up = (grad_sig * g).astype(BF16)
        grad_gate = (grad_sig * u * (1.0 + g * (1.0 - sig))).astype(BF16)
        dgu_ref[:, lo:lo + chunk] = grad_gate
        dgu_ref[:, FF + lo:FF + lo + chunk] = grad_up
        grad_normed = grad_normed + mm(grad_gate, wgu[:, lo:lo + chunk], 1, 1) + mm(grad_up, wgu[:, FF + lo:FF + lo + chunk], 1, 1)
    h32 = h_ref[...].astype(F32)
    inv_rms = inv_rms_of(h32)
    scaled = h32 * inv_rms
    part = jnp.sum(grad_normed * scaled, axis=0, keepdims=True)

    @pl.when(step == 0)
    def _():
        dgain_ref[...] = jnp.zeros_like(dgain_ref)

    dgain_ref[...] += part
    grad_scaled = grad_normed * gain_ref[...]
    dmid_ref[...] = dy.astype(F32) + inv_rms * (grad_scaled - scaled * jnp.mean(grad_scaled * scaled, axis=-1, keepdims=True))


def mlp_bwd(dy, h, g, u, gain, wgu, wd, tm=256, chunk=1280):
    tokens = h.shape[0]
    row = lambda n: pl.BlockSpec((tm, n), lambda i: (i, 0))
    return pl.pallas_call(
        functools.partial(mlp_bwd_kernel, chunk),
        grid=(tokens // tm,),
        in_specs=[row(D), row(D), row(FF), row(FF), const_spec((1, D)), const_spec((D, 2 * FF)), const_spec((FF, D))],
        out_specs=[row(2 * FF), row(D), pl.BlockSpec((1, D), lambda i: (0, 0))],
        out_shape=[jax.ShapeDtypeStruct((tokens, 2 * FF), BF16), jax.ShapeDtypeStruct((tokens, D), F32), jax.ShapeDtypeStruct((1, D), F32)],
        compiler_params=params(), cost_estimate=cost(2 * tokens * D * MW, tokens * 40000), name="mlp_bwd",
    )(dy, h, g, u, gain, wgu, wd)


def dw_gate_up_kernel(n_t, d_ref, out_ref):
    acc = mm(n_t[...], d_ref[...])
    for r in range(DEV):
        out_ref[r, :ROWS, :] = acc[r * ROWS:(r + 1) * ROWS]


def dw_down_kernel(act_t, dy_ref, _, out_ref):
    acc = mm(act_t[...], dy_ref[...])
    for d in range(acc.shape[0] // SHARD_FF):
        for i in range(20):
            for j in range(8):
                width = min(128, D - j * 128)
                out_ref[d, j * 8:(j + 1) * 8, i * 128:i * 128 + width] = acc[d * SHARD_FF + i * 8:d * SHARD_FF + (i + 1) * 8, j * 128:j * 128 + width]


def mlp_weight_grads(n_t, act_t, dgu, dy, tn=512, tm=320):
    tokens = dy.shape[0]
    pack = pl.pallas_call(
        dw_gate_up_kernel,
        grid=(2 * FF // tn,),
        in_specs=[const_spec((D, tokens)), pl.BlockSpec((tokens, tn), lambda i: (0, i))],
        out_specs=pl.BlockSpec((DEV, PAD_ROWS, tn), lambda i: (0, 0, i)),
        out_shape=jax.ShapeDtypeStruct((DEV, PAD_ROWS, MW), F32),
        compiler_params=params(), cost_estimate=cost(2 * tokens * D * 2 * FF, tokens * 12000 + D * FF * 8), name="dw_gate_up",
    )(n_t, dgu)
    return pl.pallas_call(
        dw_down_kernel,
        grid=(FF // tm,),
        in_specs=[pl.BlockSpec((tm, tokens), lambda i: (i, 0)), const_spec((tokens, D)), ANY],
        out_specs=pl.BlockSpec((tm // SHARD_FF, PAD_ROWS, FF), lambda i: (i, 0, 2)),
        out_shape=jax.ShapeDtypeStruct((DEV, PAD_ROWS, MW), F32),
        input_output_aliases={2: 0},
        compiler_params=params(), cost_estimate=cost(2 * tokens * D * FF, tokens * 7000 + D * FF * 4), name="dw_down",
    )(act_t, dy, pack)


def attn_bwd_kernel(seqs, dmid_ref, x_ref, qkv_ref, o_ref, gain_ref, dgain_mlp_ref, cos_ref, sin_ref, wqkv_t, wo,
                    dx_ref, pack_ref, do_t, dqkv_t, dwqkv_t, dwo, dgain):
    step = pl.program_id(0)

    @pl.when(step == 0)
    def _():
        dwqkv_t[...] = jnp.zeros_like(dwqkv_t)
        dwo[...] = jnp.zeros_like(dwo)
        dgain[...] = jnp.zeros_like(dgain)

    grad_mid = dmid_ref[...]
    grad_mid_bf = grad_mid.astype(BF16)
    dwo[...] += mm(o_ref[...], grad_mid_bf)
    do_t[...] = mm(wo[...], grad_mid_bf, 1, 1).astype(BF16)
    cos, sin = cos_ref[...], sin_ref[...]
    half = HD // 2

    def unrotate(grad, row, cols):
        a, b = grad[:half], grad[half:]
        c, s = cos[:, :SEQ], sin[:, :SEQ]
        dqkv_t[row:row + half, cols] = (a * c + b * s).astype(BF16)
        dqkv_t[row + half:row + HD, cols] = (b * c - a * s).astype(BF16)

    for seq in range(seqs):
        cols = slice(seq * SEQ, (seq + 1) * SEQ)
        for kvh in range(KVH):
            k_t = qkv_ref[D + kvh * HD:D + (kvh + 1) * HD, cols]
            v_t = qkv_ref[D + KV + kvh * HD:D + KV + (kvh + 1) * HD, cols]
            q_t = group_cols(qkv_ref, kvh, seq)
            g_t = group_cols(do_t, kvh, seq)
            p_t = probs_t(k_t, q_t)
            dqkv_t[D + KV + kvh * HD:D + KV + (kvh + 1) * HD, cols] = mm(g_t, p_t, 1, 1).astype(BF16)
            dp_t = mm(v_t.T, g_t)
            p32 = p_t.astype(F32)
            ds_t = (p32 * (dp_t - jnp.sum(p32 * dp_t, axis=0, keepdims=True)) * HD ** -0.5).astype(BF16)
            dq_t = mm(k_t, ds_t)
            for g in range(GROUP):
                unrotate(dq_t[:, g * SEQ:(g + 1) * SEQ], (kvh * GROUP + g) * HD, cols)
            unrotate(mm(q_t, ds_t, 1, 1), D + kvh * HD, cols)

    x32 = x_ref[...].astype(F32)
    inv_rms = inv_rms_of(x32)
    scaled = x32 * inv_rms
    normed = (scaled * gain_ref[...]).astype(BF16)
    dwqkv_t[...] += mm(dqkv_t[...], normed)
    grad_normed = mm(dqkv_t[...].T, wqkv_t[...])
    dgain[...] += jnp.sum(grad_normed * scaled, axis=0, keepdims=True)
    grad_scaled = grad_normed * gain_ref[...]
    dx_ref[...] = (grad_mid + inv_rms * (grad_scaled - scaled * jnp.mean(grad_scaled * scaled, axis=-1, keepdims=True))).astype(BF16)

    @pl.when(step == pl.num_programs(0) - 1)
    def _():
        for lo in range(0, QKV, KV):
            part = dwqkv_t[lo:lo + KV, :].T
            for r in range(DEV):
                pack_ref[r, :ROWS, lo:lo + KV] = part[r * ROWS:(r + 1) * ROWS]
        for r in range(DEV):
            pack_ref[r, :ROWS, QKV:AW] = dwo[r * ROWS:(r + 1) * ROWS, :]
            pack_ref[r, ROWS:ROWS + 1, :ROWS] = dgain[:, r * ROWS:(r + 1) * ROWS]
            pack_ref[r, ROWS + 1:ROWS + 2, :ROWS] = dgain_mlp_ref[:, r * ROWS:(r + 1) * ROWS]


def attn_bwd(dmid, x, qkv_t, o_t, gain, dgain_mlp, cos_t, sin_t, wqkv_t, wo, seqs=2):
    tokens = x.shape[0]
    tm = seqs * SEQ
    row = pl.BlockSpec((tm, D), lambda i: (i, 0))
    col = lambda n: pl.BlockSpec((n, tm), lambda i: (0, i))
    return pl.pallas_call(
        functools.partial(attn_bwd_kernel, seqs),
        grid=(tokens // tm,),
        in_specs=[row, row, col(QKV), col(D), const_spec((1, D)), const_spec((1, D)), const_spec((HD // 2, tm)), const_spec((HD // 2, tm)),
                  const_spec((QKV, D)), const_spec((D, D))],
        out_specs=[row, pl.BlockSpec((DEV, PAD_ROWS, GAW), lambda i: (0, 0, 0))],
        out_shape=[jax.ShapeDtypeStruct((tokens, D), BF16), jax.ShapeDtypeStruct((DEV, PAD_ROWS, GAW), F32)],
        scratch_shapes=[pltpu.VMEM((D, tm), BF16), pltpu.VMEM((QKV, tm), BF16), pltpu.VMEM((QKV, D), F32), pltpu.VMEM((D, D), F32),
                        pltpu.VMEM((1, D), F32)],
        compiler_params=params(), cost_estimate=cost(2 * tokens * D * AW * 3.2, tokens * 16000), name="attn_bwd",
    )(dmid, x, qkv_t, o_t, gain, dgain_mlp, cos_t, sin_t, wqkv_t, wo)


def solution(mesh):
    shard_spec = P(None, "fsdp")
    batch_spec = P("fsdp")

    def gather(pack):
        return lax.all_gather(pack, "fsdp", axis=0, tiled=True).reshape(DEV, PAD_ROWS, pack.shape[-1])

    def scatter(pack):
        return lax.psum_scatter(pack.reshape(DEV * PAD_ROWS, pack.shape[-1]), "fsdp", scatter_dimension=0, tiled=True)

    def step_body(w_query, w_key, w_value, w_out, w_gate, w_up, w_down, gain_attn, gain_mlp, rope_cos, rope_sin, x_in, y_cot):
        layers = w_query.shape[0]
        shape = x_in.shape
        cos_t = jnp.tile(rope_cos.T, (1, 2))
        sin_t = jnp.tile(rope_sin.T, (1, 2))
        packs = []
        for n in range(layers):
            gains = jnp.stack([jnp.pad(gain_attn[n], (0, AW - ROWS)), jnp.pad(gain_mlp[n], (0, AW - ROWS))])
            attn_rows = jnp.concatenate([w_query[n], w_key[n], w_value[n], w_out[n]], axis=-1)
            attn_pack = jnp.concatenate([attn_rows, gains, jnp.zeros((PAD_ROWS - ROWS - 2, AW), F32)], axis=0).astype(BF16)
            gate_up = jnp.pad(jnp.concatenate([w_gate[n], w_up[n]], axis=-1), ((0, PAD_ROWS - ROWS), (0, 0)))
            down = jnp.pad(w_down[n], ((0, 0), (0, 1024 - D))).reshape(10, 16, 8, 128).transpose(0, 2, 1, 3).reshape(4, 20, 16, 128)
            down = down.transpose(0, 2, 1, 3).reshape(PAD_ROWS, FF)
            mlp_pack = jnp.concatenate([gate_up, down], axis=-1).astype(BF16)
            packs.append((attn_pack, mlp_pack))
        hidden = x_in.reshape(-1, D)
        saved = []
        raw_attn, mlp_pack = lax.optimization_barrier((gather(packs[0][0]), packs[0][1]))
        raw_mlp = gather(mlp_pack)
        for n in range(layers):
            raw_attn, hidden = lax.optimization_barrier((raw_attn, hidden))
            gains = raw_attn[:, ROWS:ROWS + 2, :ROWS].astype(F32).transpose(1, 0, 2).reshape(2, 1, D)
            mid, qkv_t, o_t, wqkv_t, wo = attn_fwd(raw_attn, hidden, gains[0], cos_t, sin_t)
            next_mlp = None
            if n + 1 < layers:
                mid, next_packs = lax.optimization_barrier((mid, packs[n + 1]))
                raw_attn, next_mlp = gather(next_packs[0]), gather(next_packs[1])
            out, g, u, n_t, act_t, wgu, wd = mlp_fwd(raw_mlp, mid, gains[1])
            saved.append((hidden, gains, qkv_t, o_t, wqkv_t, wo, mid, g, u, n_t, act_t, wgu, wd))
            hidden, raw_mlp = out, next_mlp
        grad = y_cot.reshape(-1, D)
        reduced = [None] * layers
        for n in reversed(range(layers)):
            x, gains, qkv_t, o_t, wqkv_t, wo, mid, g, u, n_t, act_t, wgu, wd = saved[n]
            dgu, dmid, dgain_mlp = mlp_bwd(grad, mid, g, u, gains[1], wgu, wd)
            mlp_grads, dmid = lax.optimization_barrier((mlp_weight_grads(n_t, act_t, dgu, grad), dmid))
            mlp_sum = scatter(mlp_grads)
            grad, attn_grads = attn_bwd(dmid, x, qkv_t, o_t, gains[0], dgain_mlp, cos_t, sin_t, wqkv_t, wo)
            attn_sum = scatter(attn_grads)
            reduced[n] = (attn_sum, mlp_sum)

        def collect(pick):
            return jnp.stack([pick(*parts) for parts in reduced])

        def down_rows(m):
            return m[:, 2 * FF:].reshape(8, 8, 20, 128).transpose(2, 1, 0, 3).reshape(SHARD_FF, 1024)[:, :D]

        return (
            hidden.reshape(shape), grad.reshape(shape),
            collect(lambda a, m: a[:ROWS, :D]),
            collect(lambda a, m: a[:ROWS, D:D + KV]),
            collect(lambda a, m: a[:ROWS, D + KV:QKV]),
            collect(lambda a, m: a[:ROWS, QKV:AW]),
            collect(lambda a, m: m[:ROWS, :FF]),
            collect(lambda a, m: m[:ROWS, FF:2 * FF]),
            collect(lambda a, m: down_rows(m)),
            collect(lambda a, m: a[ROWS, :ROWS]),
            collect(lambda a, m: a[ROWS + 1, :ROWS]),
        )

    in_specs = (shard_spec,) * 9 + (P(), P(), batch_spec, batch_spec)
    out_specs = (batch_spec, batch_spec) + (shard_spec,) * 9
    return jax.shard_map(step_body, mesh=mesh, in_specs=in_specs, out_specs=out_specs, check_vma=False)
```

time: 2770 us -> 1430 us (0.52)
  matrix products: 1330 us -> 0 us
  blocking collectives: 958 us -> 0 us
  Pallas kernels: 0 us -> 887 us
  waiting for transfers between devices: 5.69 us -> 428 us
  other arithmetic: 253 us -> 9.48 us
  local copies, waits for them, and re-layouts: 159 us -> 83.8 us
  starting transfers between devices: 33.9 us -> 0.32 us
    dot_general x52 -> x0, matrix products: 1270 us -> none  [the longest x2 132 us: layer_backward(): jnp.einsum('bkgqs,bskd->bqkgd', grad_scores, k_heads, preferred_element_t...]
    pallas_call x0 -> x12, Pallas kernels: none -> 887 us  [the longest x2 239 us: attn_bwd(): pl.pallas_call(functools.partial(attn_bwd_kernel, seqs), grid=(tokens //...]
    unnamed x5 -> x0, blocking collectives: 821 us -> none
    reduce_scatter x2 -> x4, waiting for transfers between devices: 0.01 us -> 388 us  [scatter(): lax.psum_scatter(pack.reshape(DEV * PAD_ROWS, pack.shape[-1]), 'fsdp', sc...]
    all_gather x8 -> x0, blocking collectives: 137 us -> none  [gather_layer(): lax.all_gather(master[layer_idx].astype(jnp.bfloat16), 'fsdp', axis=0, ti...]
    convert_element_type x16 -> x0, other arithmetic: 119 us -> none  [the longest x2 64.2 us: layer_forward(): attn_probs = jax.nn.softmax(scores, axis=-1).astype(jnp.bfloat16)]
    all_gather x12 -> x0, local copies, waits for them, and re-layouts: 72 us -> none  [gather_layer(): lax.all_gather(master[layer_idx].astype(jnp.bfloat16), 'fsdp', axis=0, ti...]
    sub x2 -> x0, matrix products: 59.2 us -> none  [layer_forward(): attn_probs = jax.nn.softmax(scores, axis=-1).astype(jnp.bfloat16)]
  transfers between devices with their start and end apart: 34 -> 8, of which waited for: 0 -> 4; matrix products, arithmetic and copies ran while one was open for 88% -> 5% of each run, Pallas kernels for 0% -> 36%
where the time goes in v1:
time: 1430 us; the launch traced here: 1420 us
  Pallas kernels  887 us (62%)
  waiting for transfers between devices  428 us (30%)
  local copies, waits for them, and re-layouts  83.8 us (6%)
  between operations  14.9 us (1%)
    reduce_scatter x4, waiting for transfers between devices, scatter(): lax.psum_scatter(pack.reshape(DEV * PAD_ROWS, pack.shape[-1]), 'fsdp', sc...  388 us
    pallas_call x2, Pallas kernels, attn_bwd(): pl.pallas_call(functools.partial(attn_bwd_kernel, seqs), grid=(tokens //...  239 us
    pallas_call x2, Pallas kernels, mlp_bwd(): pl.pallas_call(functools.partial(mlp_bwd_kernel, chunk), grid=(tokens //...  180 us
    pallas_call x2, Pallas kernels, mlp_fwd(): pl.pallas_call(functools.partial(mlp_fwd_kernel, chunk), grid=(tokens //...  175 us
    pallas_call x2, Pallas kernels, attn_fwd(): pl.pallas_call(functools.partial(attn_fwd_kernel, seqs), grid=(tokens //...  140 us
    pallas_call x2, Pallas kernels, mlp_weight_grads(): pl.pallas_call(dw_gate_up_kernel, grid=(2 * FF // tn,), in_specs=[const_s...  96.4 us
    unnamed x33, local copies, waits for them, and re-layouts  65.5 us
    pallas_call x2, Pallas kernels, mlp_weight_grads(): pl.pallas_call(dw_down_kernel, grid=(FF // tm,), in_specs=[pl.BlockSpec((...  56.7 us
  transfers between devices with their start and end apart: 8, of which 4 were waited for; matrix products, arithmetic and copies ran while one was open for 5% of the time, Pallas kernels for 36%

profile of v1, /device:TPU:0, one launch (start us, length us, event | category | flops | bytes accessed | tf_op | source)
XLA Modules:
  0.0 1423.5 jit_solution(6234331102464279763)
XLA Ops:
  13.0 1.2 copy.105
  14.2 1.2 copy.104
  17.9 1.8 maximum_maximum_fusion.1
  20.0 1.5 copy.102
  23.2 38.2 %all-gather.5.cloned.1.call-done = bf16[1024,2560]{1,0:T(8,128)(2,1)} async-done(((bf16[64,2560]{1,0:T(8,128)(2,1)}), bf16[1024,2560]{1,0:T(8,128)(2,1)}) %all-gather.5.cloned.1.call-update) | async-done | bytes 5242896 | tf_op jit(solution)/shard_map/all_gather | solution.py:373
  63.2 12.2 copy.72
  77.9 70.0 %attn_fwd.2 = (bf16[4096,960]{1,0:T(8,128)(2,1)}, bf16[1600,4096]{1,0:T(8,128)(2,1)}, bf16[960,4096]{1,0:T(8,128)(2,1)}, bf16[1600,960]{1,0:T(8,128)(2,1)}, bf16[960,960]{1,0:T(8,128)(2,1)}) custom-call(bf16[16,64,2560]{2,1,0:T(8,128)(2,1)} %bitcast.163, bf16[4096,960]{1,0:T(8,128)(2,1)} %bitcast.138, f32[1,960]{1,0:T(1,128)} %squeeze.97.gain_ref, ...), custom_call_target="tpu_custom_call" | custom-call | flops 32212254720 | bytes 32768000 | tf_op jit(solution)/shard_map/attn_fwd/pallas_call | solution.py:138
  148.6 12.5 copy.75
  161.8 87.4 %mlp_fwd.2 = (bf16[4096,960]{1,0:T(8,128)(2,1)}, f32[4096,2560]{1,0:T(8,128)}, f32[4096,2560]{1,0:T(8,128)}, bf16[960,4096]{1,0:T(8,128)(2,1)}, bf16[2560,4096]{...) custom-call(bf16[16,64,7680]{2,1,0:T(8,128)(2,1)} %bitcast.166, ...), custom_call_target="tpu_custom_call" | custom-call | flops 60397977600 | bytes 122880000 | tf_op jit(solution)/shard_map/mlp_fwd/pallas_call | solution.py:196
  251.4 69.9 %attn_fwd.3 = (bf16[4096,960]{1,0:T(8,128)(2,1)}, bf16[1600,4096]{1,0:T(8,128)(2,1)}, bf16[960,4096]{1,0:T(8,128)(2,1)}, bf16[1600,960]{1,0:T(8,128)(2,1)}, bf16[960,960]{1,0:T(8,128)(2,1)}) custom-call(bf16[16,64,2560]{2,1,0:T(8,128)(2,1)} %bitcast.165, bf16[4096,960]{1,0:T(8,128)(2,1)} %get-tuple-element.68.x_ref, f32[1,960]{1,0:T(1,128)} %squeeze.108.gain_ref, ...), custom_call_target="tpu_custom_call" | custom-call | flops 32212254720 | bytes 32768000 | tf_op jit(solution)/shard_map/attn_fwd/pallas_call | solution.py:138
  321.3 87.3 %mlp_fwd.3 = (bf16[4096,960]{1,0:T(8,128)(2,1)}, f32[4096,2560]{1,0:T(8,128)}, f32[4096,2560]{1,0:T(8,128)}, bf16[960,4096]{1,0:T(8,128)(2,1)}, bf16[2560,4096]{...) custom-call(bf16[16,64,7680]{2,1,0:T(8,128)(2,1)} %bitcast.167, ...), custom_call_target="tpu_custom_call" | custom-call | flops 60397977600 | bytes 122880000 | tf_op jit(solution)/shard_map/mlp_fwd/pallas_call | solution.py:196
  408.6 89.6 %mlp_bwd.2 = (bf16[4096,5120]{1,0:T(8,128)(2,1)}, f32[4096,960]{1,0:T(8,128)}, f32[1,960]{1,0:T(1,128)}) custom-call(bf16[4096,960]{1,0:T(8,128)(2,1)} %bitcast.134, bf16[4096,960]{1,0:T(8,128)(2,1)} %get-tuple-element.69.h_ref, f32[4096,2560]{1,0:T(8,128)} %get-tuple-element.74.g_ref, f32[4096,2560]{1,0:T(8,128)} %get-tuple-element.75.u_ref, ...), custom_call_target="tpu_custom_call" | custom-call | flops 60397977600 | bytes 163840000 | tf_op jit(solution)/shard_map/mlp_bwd/pallas_call | solution.py:242
  498.2 48.2 %dw_gate_up.2._ = f32[16,64,7680]{2,1,0:T(8,128)} custom-call(bf16[960,4096]{1,0:T(8,128)(2,1)} %get-tuple-element.73.n_t, bf16[4096,5120]{1,0:T(8,128)(2,1)} %get-tuple-element.78.d_ref), custom_call_target="tpu_custom_call" | custom-call | flops 40265318400 | bytes 68812800 | tf_op jit(solution)/shard_map/dw_gate_up/pallas_call | solution.py:269
  546.4 28.3 %dw_down.2 = f32[16,64,7680]{2,1,0:T(8,128)} custom-call(bf16[2560,4096]{1,0:T(8,128)(2,1)} %get-tuple-element.72.act_t, bf16[4096,960]{1,0:T(8,128)(2,1)} %bitcast.135, f32[16,64,7680]{2,1,0:T(8,128)} %dw_gate_up.2._), custom_call_target="tpu_custom_call", output_to_operand_aliasing={{}: (2, {})} | custom-call | flops 20132659200 | bytes 38502400 | tf_op jit(solution)/shard_map/dw_down/pallas_call | solution.py:277
  574.7 119.5 %attn_bwd.2 = (bf16[4096,960]{1,0:T(8,128)(2,1)}, f32[16,64,2688]{2,1,0:T(8,128)}) custom-call(f32[4096,960]{1,0:T(8,128)} %get-tuple-element.80.dmid_ref, bf16[4096,960]{1,0:T(8,128)(2,1)} %get-tuple-element.68.x_ref, bf16[1600,4096]{1,0:T(8,128)(2,1)} %get-tuple-element.81.qkv_ref, bf16[960,4096]{1,0:T(8,128)(2,1)} %get-tuple-element.82.o_ref, ...), custom_call_target="tpu_custom_call" | custom-call | flops 64424509440 | bytes 65536000 | tf_op jit(solution)/shard_map/attn_bwd/pallas_call | solution.py:355
  694.2 90.8 %mlp_bwd.3 = (bf16[4096,5120]{1,0:T(8,128)(2,1)}, f32[4096,960]{1,0:T(8,128)}, f32[1,960]{1,0:T(1,128)}) custom-call(bf16[4096,960]{1,0:T(8,128)(2,1)} %get-tuple-element.86.dy_ref, bf16[4096,960]{1,0:T(8,128)(2,1)} %get-tuple-element.65.h_ref, f32[4096,2560]{1,0:T(8,128)} %get-tuple-element.88.g_ref, f32[4096,2560]{1,0:T(8,128)} %get-tuple-element.89.u_ref, ...), custom_call_target="tpu_custom_call" | custom-call | flops 60397977600 | bytes 163840000 | tf_op jit(solution)/shard_map/mlp_bwd/pallas_call | solution.py:242
  785.0 48.2 %dw_gate_up.3._ = f32[16,64,7680]{2,1,0:T(8,128)} custom-call(bf16[960,4096]{1,0:T(8,128)(2,1)} %get-tuple-element.87.n_t, bf16[4096,5120]{1,0:T(8,128)(2,1)} %get-tuple-element.92.d_ref), custom_call_target="tpu_custom_call" | custom-call | flops 40265318400 | bytes 68812800 | tf_op jit(solution)/shard_map/dw_gate_up/pallas_call | solution.py:269
  833.3 28.4 %dw_down.3 = f32[16,64,7680]{2,1,0:T(8,128)} custom-call(bf16[2560,4096]{1,0:T(8,128)(2,1)} %get-tuple-element.71.act_t, bf16[4096,960]{1,0:T(8,128)(2,1)} %get-tuple-element.86.dy_ref, f32[16,64,7680]{2,1,0:T(8,128)} %dw_gate_up.3._), custom_call_target="tpu_custom_call", output_to_operand_aliasing={{}: (2, {})} | custom-call | flops 20132659200 | bytes 38502400 | tf_op jit(solution)/shard_map/dw_down/pallas_call | solution.py:277
  861.6 119.4 %attn_bwd.3 = (bf16[4096,960]{1,0:T(8,128)(2,1)}, f32[16,64,2688]{2,1,0:T(8,128)}) custom-call(f32[4096,960]{1,0:T(8,128)} %get-tuple-element.94.dmid_ref, bf16[4096,960]{1,0:T(8,128)(2,1)} %bitcast.139, bf16[1600,4096]{1,0:T(8,128)(2,1)} %get-tuple-element.95.qkv_ref, bf16[960,4096]{1,0:T(8,128)(2,1)} %get-tuple-element.96.o_ref, ...), custom_call_target="tpu_custom_call" | custom-call | flops 64424509440 | bytes 65536000 | tf_op jit(solution)/shard_map/attn_bwd/pallas_call | solution.py:355
  982.6 12.4 copy.78
  995.0 12.5 copy.79
  1007.5 1.2 slice_bitcast_fusion.14
  1008.7 58.2 %reduce-scatter.5.cloned.1.call-done = f32[64,2688]{1,0:T(8,128)} async-done(((f32[1024,2688]{1,0:T(8,128)}), f32[64,2688]{1,0:T(8,128)}) %reduce-scatter.5.cloned.1.call-update) | async-done | bytes 688144 | tf_op jit(solution)/shard_map/reduce_scatter | solution.py:376
  1066.9 1.2 slice_bitcast_fusion.15
  1068.1 1.2 copy.83
  1073.1 1.2 copy.80
  1076.9 161.2 %reduce-scatter.11.cloned.1.call-done = f32[64,7680]{1,0:T(8,128)} async-done(((f32[1024,7680]{1,0:T(8,128)}), f32[64,7680]{1,0:T(8,128)}) %reduce-scatter.11.cloned.1.call-update) | async-done | bytes 1966096 | tf_op jit(solution)/shard_map/reduce_scatter | solution.py:376
  1238.2 1.3 copy_bitcast_fusion
  1240.0 168.5 %reduce-scatter.9.cloned.1.call-done = f32[64,7680]{1,0:T(8,128)} async-done(((f32[1024,7680]{1,0:T(8,128)}), f32[64,7680]{1,0:T(8,128)}) %reduce-scatter.9.cloned.1.call-update) | async-done | bytes 1966096 | tf_op jit(solution)/shard_map/reduce_scatter | solution.py:376
  1408.5 1.4 slice_bitcast_fusion.5
  1410.0 2.0 copy.85
  1413.3 2.0 copy.84
  (100 shorter events, 29.1 us)
Async XLA Ops:
  7.2 54.3 %all-gather.5.cloned.1.call-start = ((), (), s32[]{:S(2)}) async-start(), calls=%async_computation.4 | async-start | bytes 5570560 | tf_op jit(solution)/shard_map/all_gather | solution.py:373
  11.1 8.8 copy-start.2
  16.7 4.8 copy-start.1
  19.8 142.0 %all-gather.11.cloned.1.call-start = ((), (), s32[]{:S(2)}) async-start(), calls=%async_computation.7 | async-start | bytes 16711680 | tf_op jit(solution)/shard_map/all_gather | solution.py:373
  22.0 39.5 %copy-start.3 = (f32[256,32]{0,1:T(8,128)S(1)}, f32[256,32]{0,1:T(8,128)}, u32[]{:S(2)}) copy-start(f32[256,32]{0,1:T(8,128)} %param.22) | copy-start | bytes 98308
  22.1 40.1 %copy-start.4 = (f32[256,32]{0,1:T(8,128)S(1)}, f32[256,32]{0,1:T(8,128)}, u32[]{:S(2)}) copy-start(f32[256,32]{0,1:T(8,128)} %param.23) | copy-start | bytes 98308
  61.5 187.7 %all-gather.9.cloned.1.call-start = ((), (), s32[]{:S(2)}) async-start(), calls=%async_computation.6 | async-start | bytes 5570560 | tf_op jit(solution)/shard_map/all_gather | solution.py:373
  147.9 173.4 %all-gather.7.cloned.1.call-start = ((), (), s32[]{:S(2)}) async-start(), calls=%async_computation.5 | async-start | bytes 16711680 | tf_op jit(solution)/shard_map/all_gather | solution.py:373
  148.5 859.0 %reduce-scatter.7.cloned.1.call-start = ((), (), s32[]{:S(2)}) async-start(), calls=%async_computation.9 | async-start | bytes 11698176 | tf_op jit(solution)/shard_map/reduce_scatter | solution.py:376
  694.2 372.7 %reduce-scatter.5.cloned.1.call-start = ((), (), s32[]{:S(2)}) async-start(), calls=%async_computation.8 | async-start | bytes 11698176 | tf_op jit(solution)/shard_map/reduce_scatter | solution.py:376
  981.1 257.1 %reduce-scatter.11.cloned.1.call-start = ((), (), s32[]{:S(2)}) async-start(), calls=%async_computation.11 | async-start | bytes 33423360 | tf_op jit(solution)/shard_map/reduce_scatter | solution.py:376
  981.8 426.7 %reduce-scatter.9.cloned.1.call-start = ((), (), s32[]{:S(2)}) async-start(), calls=%async_computation.10 | async-start | bytes 33423360 | tf_op jit(solution)/shard_map/reduce_scatter | solution.py:376
  1238.2 1.7 copy-start
Sparse Core Ops, SparseCore 0:
  19.9 41.5 all-gather.4
  64.3 72.9 all-gather.10
  148.1 38.7 all-gather.8
  189.5 72.9 all-gather.6
  694.3 85.7 reduce-scatter.6
  981.2 85.6 reduce-scatter.4
  1071.8 166.3 reduce-scatter.10
  1243.0 165.4 reduce-scatter.8

commit v2 on v1

--- a/solution.py
+++ b/solution.py
@@ -26,7 +26,8 @@
 SEQ = 256
 QKV = D + 2 * KV
 AW = QKV + D
-GAW = 2688
+GW = 5376
+GW1 = 2688
 MW = 3 * FF
 VMEM_LIMIT = 62 * 1024 * 1024
 EXP_SCALE = HD ** -0.5 * 1.4426950408889634
@@ -50,6 +51,30 @@
 
 
 ANY = pl.BlockSpec(memory_space=pl.ANY)
+
+
+def load_tokens(ref):
+    if len(ref.shape) == 2:
+        return ref[...]
+    return jnp.concatenate([ref[i].T for i in range(ref.shape[0])], axis=0)
+
+
+def store_tokens(ref, vals):
+    if len(ref.shape) == 2:
+        ref[...] = vals
+    else:
+        for i in range(ref.shape[0]):
+            ref[i] = vals[i * SEQ:(i + 1) * SEQ].T
+
+
+def token_spec(tm, transposed):
+    if transposed:
+        return pl.BlockSpec((tm // SEQ, D, SEQ), lambda i: (i, 0, 0))
+    return pl.BlockSpec((tm, D), lambda i: (i, 0))
+
+
+def token_shape(tokens, transposed):
+    return jax.ShapeDtypeStruct((tokens // SEQ, D, SEQ) if transposed else (tokens, D), BF16)
 
 
 def inv_rms_of(vals32):
@@ -68,18 +93,32 @@
         place(d, buf.at[d % 2])
 
 
-def probs_t(k_t, q_t):
-    scores = mm(k_t.T, q_t) * EXP_SCALE
+HALF_SEQ = SEQ // 2
+
+
+def group_cols(ref, kv_head, seq, part):
+    base, lo = kv_head * GROUP * HD, seq * SEQ + part * HALF_SEQ
+    return jnp.concatenate([ref[base + g * HD: base + (g + 1) * HD, lo:lo + HALF_SEQ] for g in range(GROUP)], axis=1)
+
+
+def causal(scores):
     key = lax.broadcasted_iota(jnp.int32, scores.shape, 0)
-    qry = lax.broadcasted_iota(jnp.int32, scores.shape, 1) & (SEQ - 1)
-    scores = jnp.where(key <= qry, scores, MASK_VALUE)
-    exps = jnp.exp2(scores - jnp.max(scores, axis=0, keepdims=True))
-    return (exps * (1.0 / jnp.sum(exps, axis=0, keepdims=True))).astype(BF16)
-
-
-def group_cols(ref, kv_head, seq):
-    base = kv_head * GROUP * HD
-    return jnp.concatenate([ref[base + g * HD: base + (g + 1) * HD, seq * SEQ:(seq + 1) * SEQ] for g in range(GROUP)], axis=1)
+    qry = lax.broadcasted_iota(jnp.int32, scores.shape, 1) & (HALF_SEQ - 1)
+    return jnp.where(key <= qry, scores, MASK_VALUE)
+
+
+def score_pair(keys, q_a, q_b):
+    return mm(keys[:HALF_SEQ], q_a), mm(keys, q_b)
+
+
+def prob_pair(scores):
+    s_a = causal(scores[0] * EXP_SCALE)
+    e_a = jnp.exp2(s_a - jnp.max(s_a, axis=0, keepdims=True))
+    p_a = (e_a * (1.0 / jnp.sum(e_a, axis=0, keepdims=True))).astype(BF16)
+    s_b = jnp.concatenate([scores[1][:HALF_SEQ] * EXP_SCALE, causal(scores[1][HALF_SEQ:] * EXP_SCALE)], axis=0)
+    e_b = jnp.exp2(s_b - jnp.max(s_b, axis=0, keepdims=True))
+    p_b = (e_b * (1.0 / jnp.sum(e_b, axis=0, keepdims=True))).astype(BF16)
+    return p_a, p_b
 
 
 def attn_fwd_kernel(seqs, raw, x_ref, gain_ref, cos_ref, sin_ref, h_ref, qkv_ref, o_ref, wqkv_out, wo_out,
@@ -98,7 +137,7 @@
         for copy in copies:
             copy.start()
 
-    x32 = x_ref[...].astype(F32)
+    x32 = load_tokens(x_ref).astype(F32)
     normed = (x32 * inv_rms_of(x32) * gain_ref[...]).astype(BF16)
     cos, sin = cos_ref[...], sin_ref[...]
     half = HD // 2
@@ -112,16 +151,24 @@
                 qkv_ref[lo + head * HD + half:lo + (head + 1) * HD, :] = (b * cos + a * sin).astype(BF16)
         else:
             qkv_ref[lo:lo + KV, :] = part.astype(BF16)
-    for seq in range(seqs):
-        cols = slice(seq * SEQ, (seq + 1) * SEQ)
-        for kvh in range(KVH):
-            k_t = qkv_ref[D + kvh * HD:D + (kvh + 1) * HD, cols]
-            v_t = qkv_ref[D + KV + kvh * HD:D + KV + (kvh + 1) * HD, cols]
-            p_t = probs_t(k_t, group_cols(qkv_ref, kvh, seq))
-            o_t = mm(v_t, p_t).astype(BF16)
+    items = [(seq, kvh) for seq in range(seqs) for kvh in range(KVH)]
+
+    def scores_of(seq, kvh):
+        keys = qkv_ref[D + kvh * HD:D + (kvh + 1) * HD, seq * SEQ:(seq + 1) * SEQ].T
+        return score_pair(keys, group_cols(qkv_ref, kvh, seq, 0), group_cols(qkv_ref, kvh, seq, 1))
+
+    scores = scores_of(*items[0])
+    for pos, (seq, kvh) in enumerate(items):
+        ahead = scores_of(*items[pos + 1]) if pos + 1 < len(items) else None
+        probs = prob_pair(scores)
+        scores = ahead
+        v_t = qkv_ref[D + KV + kvh * HD:D + KV + (kvh + 1) * HD, seq * SEQ:(seq + 1) * SEQ]
+        for part in range(2):
+            o_t = mm(v_t[:, :(part + 1) * HALF_SEQ], probs[part]).astype(BF16)
+            lo = seq * SEQ + part * HALF_SEQ
             for g in range(GROUP):
                 row = (kvh * GROUP + g) * HD
-                o_ref[row:row + HD, cols] = o_t[:, g * SEQ:(g + 1) * SEQ]
+                o_ref[row:row + HD, lo:lo + HALF_SEQ] = o_t[:, g * HALF_SEQ:(g + 1) * HALF_SEQ]
     h_ref[...] = (x32 + mm(o_ref[...].T, wo[...])).astype(BF16)
 
     @pl.when(step == pl.num_programs(0) - 1)
@@ -131,14 +178,14 @@
 
 
 def attn_fwd(raw, x, gain, cos_t, sin_t, seqs=2):
-    tokens = x.shape[0]
+    tokens = x.size // D
     tm = seqs * SEQ
     row = pl.BlockSpec((tm, D), lambda i: (i, 0))
     col = lambda n: pl.BlockSpec((n, tm), lambda i: (0, i))
     return pl.pallas_call(
         functools.partial(attn_fwd_kernel, seqs),
         grid=(tokens // tm,),
-        in_specs=[ANY, row, const_spec((1, D)), const_spec((HD // 2, tm)), const_spec((HD // 2, tm))],
+        in_specs=[ANY, token_spec(tm, x.ndim == 3), const_spec((1, D)), const_spec((HD // 2, tm)), const_spec((HD // 2, tm))],
         out_specs=[row, col(QKV), col(D), ANY, ANY],
         out_shape=[jax.ShapeDtypeStruct((tokens, D), BF16), jax.ShapeDtypeStruct((QKV, tokens), BF16),
                    jax.ShapeDtypeStruct((D, tokens), BF16), jax.ShapeDtypeStruct((QKV, D), BF16), jax.ShapeDtypeStruct((D, D), BF16)],
@@ -171,7 +218,6 @@
     h32 = h_ref[...].astype(F32)
     normed = (h32 * inv_rms_of(h32) * gain_ref[...]).astype(BF16)
     n_ref[...] = normed.T
-    y_ref[...] = h_ref[...]
     out = h32
     for lo in range(0, FF, chunk):
         g = mm(normed, wgu[:, lo:lo + chunk])
@@ -181,7 +227,7 @@
         act = (g * (0.5 * jnp.tanh(0.5 * g) + 0.5) * u).astype(BF16)
         act_ref[lo:lo + chunk, :] = act.T
         out = out + mm(act, wd[lo:lo + chunk, :])
-    y_ref[...] = out.astype(BF16)
+    store_tokens(y_ref, out.astype(BF16))
 
     @pl.when(step == pl.num_programs(0) - 1)
     def _():
@@ -189,7 +235,7 @@
             copy.wait()
 
 
-def mlp_fwd(raw, h, gain, tm=256, chunk=1280):
+def mlp_fwd(raw, h, gain, transposed, tm=256, chunk=1280):
     tokens = h.shape[0]
     row = lambda n: pl.BlockSpec((tm, n), lambda i: (i, 0))
     col = lambda n: pl.BlockSpec((n, tm), lambda i: (0, i))
@@ -197,8 +243,8 @@
         functools.partial(mlp_fwd_kernel, chunk),
         grid=(tokens // tm,),
         in_specs=[ANY, row(D), const_spec((1, D))],
-        out_specs=[row(D), row(FF), row(FF), col(D), col(FF), ANY, ANY],
-        out_shape=[jax.ShapeDtypeStruct((tokens, D), BF16), jax.ShapeDtypeStruct((tokens, FF), F32), jax.ShapeDtypeStruct((tokens, FF), F32),
+        out_specs=[token_spec(tm, transposed), row(FF), row(FF), col(D), col(FF), ANY, ANY],
+        out_shape=[token_shape(tokens, transposed), jax.ShapeDtypeStruct((tokens, FF), F32), jax.ShapeDtypeStruct((tokens, FF), F32),
                    jax.ShapeDtypeStruct((D, tokens), BF16), jax.ShapeDtypeStruct((FF, tokens), BF16),
                    jax.ShapeDtypeStruct((D, 2 * FF), BF16), jax.ShapeDtypeStruct((FF, D), BF16)],
         scratch_shapes=[pltpu.VMEM((2, PAD_ROWS, MW), BF16), pltpu.VMEM((D, 2 * FF), BF16), pltpu.VMEM((FF, D), BF16),
@@ -209,7 +255,7 @@
 
 def mlp_bwd_kernel(chunk, dy_ref, h_ref, g_ref, u_ref, gain_ref, wgu, wd, dgu_ref, dmid_ref, dgain_ref):
     step = pl.program_id(0)
-    dy = dy_ref[...]
+    dy = load_tokens(dy_ref)
     grad_normed = jnp.zeros((dy.shape[0], D), F32)
     for lo in range(0, FF, chunk):
         grad_act = mm(dy, wd[lo:lo + chunk, :], 1, 1)
@@ -242,7 +288,7 @@
     return pl.pallas_call(
         functools.partial(mlp_bwd_kernel, chunk),
         grid=(tokens // tm,),
-        in_specs=[row(D), row(D), row(FF), row(FF), const_spec((1, D)), const_spec((D, 2 * FF)), const_spec((FF, D))],
+        in_specs=[token_spec(tm, dy.ndim == 3), row(D), row(FF), row(FF), const_spec((1, D)), const_spec((D, 2 * FF)), const_spec((FF, D))],
         out_specs=[row(2 * FF), row(D), pl.BlockSpec((1, D), lambda i: (0, 0))],
         out_shape=[jax.ShapeDtypeStruct((tokens, 2 * FF), BF16), jax.ShapeDtypeStruct((tokens, D), F32), jax.ShapeDtypeStruct((1, D), F32)],
         compiler_params=params(), cost_estimate=cost(2 * tokens * D * MW, tokens * 40000), name="mlp_bwd",
@@ -255,8 +301,17 @@
         out_ref[r, :ROWS, :] = acc[r * ROWS:(r + 1) * ROWS]
 
 
-def dw_down_kernel(act_t, dy_ref, _, out_ref):
-    acc = mm(act_t[...], dy_ref[...])
+def dw_down_kernel(turned, act_t, dy_ref, *refs):
+    if turned:
+        out_ref, rows = refs[-2:]
+
+        @pl.when(pl.program_id(0) == 0)
+        def _():
+            for i in range(dy_ref.shape[0]):
+                rows[i * SEQ:(i + 1) * SEQ, :] = dy_ref[i].T
+    else:
+        out_ref, rows = refs[-1], dy_ref
+    acc = mm(act_t[...], rows[...])
     for d in range(acc.shape[0] // SHARD_FF):
         for i in range(20):
             for j in range(8):
@@ -264,25 +319,31 @@
                 out_ref[d, j * 8:(j + 1) * 8, i * 128:i * 128 + width] = acc[d * SHARD_FF + i * 8:d * SHARD_FF + (i + 1) * 8, j * 128:j * 128 + width]
 
 
-def mlp_weight_grads(n_t, act_t, dgu, dy, tn=512, tm=320):
-    tokens = dy.shape[0]
-    pack = pl.pallas_call(
+def dw_gate_up(n_t, dgu, tn=512):
+    tokens = dgu.shape[0]
+    return pl.pallas_call(
         dw_gate_up_kernel,
         grid=(2 * FF // tn,),
         in_specs=[const_spec((D, tokens)), pl.BlockSpec((tokens, tn), lambda i: (0, i))],
         out_specs=pl.BlockSpec((DEV, PAD_ROWS, tn), lambda i: (0, 0, i)),
-        out_shape=jax.ShapeDtypeStruct((DEV, PAD_ROWS, MW), F32),
+        out_shape=jax.ShapeDtypeStruct((DEV, PAD_ROWS, GW), F32),
         compiler_params=params(), cost_estimate=cost(2 * tokens * D * 2 * FF, tokens * 12000 + D * FF * 8), name="dw_gate_up",
     )(n_t, dgu)
+
+
+def dw_down(act_t, dy, pack=None, tm=320):
+    tokens = act_t.shape[1]
+    turned, joined = dy.ndim == 3, pack is not None
     return pl.pallas_call(
-        dw_down_kernel,
+        functools.partial(dw_down_kernel, turned),
         grid=(FF // tm,),
-        in_specs=[pl.BlockSpec((tm, tokens), lambda i: (i, 0)), const_spec((tokens, D)), ANY],
-        out_specs=pl.BlockSpec((tm // SHARD_FF, PAD_ROWS, FF), lambda i: (i, 0, 2)),
-        out_shape=jax.ShapeDtypeStruct((DEV, PAD_ROWS, MW), F32),
-        input_output_aliases={2: 0},
+        in_specs=[pl.BlockSpec((tm, tokens), lambda i: (i, 0)), const_spec(dy.shape)] + [ANY] * joined,
+        out_specs=pl.BlockSpec((tm // SHARD_FF, PAD_ROWS, FF), lambda i: (i, 0, 1 if joined else 0)),
+        out_shape=jax.ShapeDtypeStruct((DEV, PAD_ROWS, GW if joined else GW1), F32),
+        input_output_aliases={2: 0} if joined else {},
+        scratch_shapes=[pltpu.VMEM((tokens, D), BF16)] * turned,
         compiler_params=params(), cost_estimate=cost(2 * tokens * D * FF, tokens * 7000 + D * FF * 4), name="dw_down",
-    )(act_t, dy, pack)
+    )(act_t, dy, *((pack,) if joined else ()))
 
 
 def attn_bwd_kernel(seqs, dmid_ref, x_ref, qkv_ref, o_ref, gain_ref, dgain_mlp_ref, cos_ref, sin_ref, wqkv_t, wo,
@@ -302,30 +363,47 @@
     cos, sin = cos_ref[...], sin_ref[...]
     half = HD // 2
 
-    def unrotate(grad, row, cols):
+    def unrotate(grad, row, lo, pos):
+        n = grad.shape[1]
         a, b = grad[:half], grad[half:]
-        c, s = cos[:, :SEQ], sin[:, :SEQ]
-        dqkv_t[row:row + half, cols] = (a * c + b * s).astype(BF16)
-        dqkv_t[row + half:row + HD, cols] = (b * c - a * s).astype(BF16)
-
-    for seq in range(seqs):
+        c, s = cos[:, pos:pos + n], sin[:, pos:pos + n]
+        dqkv_t[row:row + half, lo:lo + n] = (a * c + b * s).astype(BF16)
+        dqkv_t[row + half:row + HD, lo:lo + n] = (b * c - a * s).astype(BF16)
+
+    items = [(seq, kvh) for seq in range(seqs) for kvh in range(KVH)]
+
+    def loads(seq, kvh):
         cols = slice(seq * SEQ, (seq + 1) * SEQ)
-        for kvh in range(KVH):
-            k_t = qkv_ref[D + kvh * HD:D + (kvh + 1) * HD, cols]
-            v_t = qkv_ref[D + KV + kvh * HD:D + KV + (kvh + 1) * HD, cols]
-            q_t = group_cols(qkv_ref, kvh, seq)
-            g_t = group_cols(do_t, kvh, seq)
-            p_t = probs_t(k_t, q_t)
-            dqkv_t[D + KV + kvh * HD:D + KV + (kvh + 1) * HD, cols] = mm(g_t, p_t, 1, 1).astype(BF16)
-            dp_t = mm(v_t.T, g_t)
-            p32 = p_t.astype(F32)
-            ds_t = (p32 * (dp_t - jnp.sum(p32 * dp_t, axis=0, keepdims=True)) * HD ** -0.5).astype(BF16)
-            dq_t = mm(k_t, ds_t)
-            for g in range(GROUP):
-                unrotate(dq_t[:, g * SEQ:(g + 1) * SEQ], (kvh * GROUP + g) * HD, cols)
-            unrotate(mm(q_t, ds_t, 1, 1), D + kvh * HD, cols)
-
-    x32 = x_ref[...].astype(F32)
+        k_t = qkv_ref[D + kvh * HD:D + (kvh + 1) * HD, cols]
+        v_t = qkv_ref[D + KV + kvh * HD:D + KV + (kvh + 1) * HD, cols]
+        q = [group_cols(qkv_ref, kvh, seq, part) for part in range(2)]
+        g = [group_cols(do_t, kvh, seq, part) for part in range(2)]
+        return k_t, q, g, score_pair(k_t.T, *q), score_pair(v_t.T, *g)
+
+    def grad_scores(p, dp):
+        p32 = p.astype(F32)
+        return (p32 * (dp - jnp.sum(p32 * dp, axis=0, keepdims=True)) * HD ** -0.5).astype(BF16)
+
+    def both(lhs, rhs):
+        early, full = mm(lhs[0], rhs[0], 1, 1), mm(lhs[1], rhs[1], 1, 1)
+        return jnp.concatenate([early + full[:, :HALF_SEQ], full[:, HALF_SEQ:]], axis=1)
+
+    now = loads(*items[0])
+    for pos, (seq, kvh) in enumerate(items):
+        ahead = loads(*items[pos + 1]) if pos + 1 < len(items) else None
+        k_t, q, g, scores, dp = now
+        now = ahead
+        p = prob_pair(scores)
+        ds = [grad_scores(p[part], dp[part]) for part in range(2)]
+        lo = seq * SEQ
+        dqkv_t[D + KV + kvh * HD:D + KV + (kvh + 1) * HD, lo:lo + SEQ] = both(g, p).astype(BF16)
+        for part in range(2):
+            dq_t = mm(k_t[:, :(part + 1) * HALF_SEQ], ds[part])
+            for head in range(GROUP):
+                unrotate(dq_t[:, head * HALF_SEQ:(head + 1) * HALF_SEQ], (kvh * GROUP + head) * HD, lo + part * HALF_SEQ, part * HALF_SEQ)
+        unrotate(both(q, ds), D + kvh * HD, lo, 0)
+
+    x32 = load_tokens(x_ref).astype(F32)
     inv_rms = inv_rms_of(x32)
     scaled = x32 * inv_rms
     normed = (scaled * gain_ref[...]).astype(BF16)
@@ -333,7 +411,7 @@
     grad_normed = mm(dqkv_t[...].T, wqkv_t[...])
     dgain[...] += jnp.sum(grad_normed * scaled, axis=0, keepdims=True)
     grad_scaled = grad_normed * gain_ref[...]
-    dx_ref[...] = (grad_mid + inv_rms * (grad_scaled - scaled * jnp.mean(grad_scaled * scaled, axis=-1, keepdims=True))).astype(BF16)
+    store_tokens(dx_ref, (grad_mid + inv_rms * (grad_scaled - scaled * jnp.mean(grad_scaled * scaled, axis=-1, keepdims=True))).astype(BF16))
 
     @pl.when(step == pl.num_programs(0) - 1)
     def _():
@@ -347,18 +425,18 @@
             pack_ref[r, ROWS + 1:ROWS + 2, :ROWS] = dgain_mlp_ref[:, r * ROWS:(r + 1) * ROWS]
 
 
-def attn_bwd(dmid, x, qkv_t, o_t, gain, dgain_mlp, cos_t, sin_t, wqkv_t, wo, seqs=2):
-    tokens = x.shape[0]
+def attn_bwd(dmid, x, qkv_t, o_t, gain, dgain_mlp, cos_t, sin_t, wqkv_t, wo, width, seqs=2):
+    tokens = dmid.shape[0]
     tm = seqs * SEQ
     row = pl.BlockSpec((tm, D), lambda i: (i, 0))
     col = lambda n: pl.BlockSpec((n, tm), lambda i: (0, i))
     return pl.pallas_call(
         functools.partial(attn_bwd_kernel, seqs),
         grid=(tokens // tm,),
-        in_specs=[row, row, col(QKV), col(D), const_spec((1, D)), const_spec((1, D)), const_spec((HD // 2, tm)), const_spec((HD // 2, tm)),
-                  const_spec((QKV, D)), const_spec((D, D))],
-        out_specs=[row, pl.BlockSpec((DEV, PAD_ROWS, GAW), lambda i: (0, 0, 0))],
-        out_shape=[jax.ShapeDtypeStruct((tokens, D), BF16), jax.ShapeDtypeStruct((DEV, PAD_ROWS, GAW), F32)],
+        in_specs=[row, token_spec(tm, x.ndim == 3), col(QKV), col(D), const_spec((1, D)), const_spec((1, D)), const_spec((HD // 2, tm)),
+                  const_spec((HD // 2, tm)), const_spec((QKV, D)), const_spec((D, D))],
+        out_specs=[token_spec(tm, x.ndim == 3), pl.BlockSpec((DEV, PAD_ROWS, AW), lambda i: (0, 0, 0))],
+        out_shape=[token_shape(tokens, x.ndim == 3), jax.ShapeDtypeStruct((DEV, PAD_ROWS, width), F32)],
         scratch_shapes=[pltpu.VMEM((D, tm), BF16), pltpu.VMEM((QKV, tm), BF16), pltpu.VMEM((QKV, D), F32), pltpu.VMEM((D, D), F32),
                         pltpu.VMEM((1, D), F32)],
         compiler_params=params(), cost_estimate=cost(2 * tokens * D * AW * 3.2, tokens * 16000), name="attn_bwd",
@@ -377,7 +455,6 @@
 
     def step_body(w_query, w_key, w_value, w_out, w_gate, w_up, w_down, gain_attn, gain_mlp, rope_cos, rope_sin, x_in, y_cot):
         layers = w_query.shape[0]
-        shape = x_in.shape
         cos_t = jnp.tile(rope_cos.T, (1, 2))
         sin_t = jnp.tile(rope_sin.T, (1, 2))
         packs = []
@@ -390,7 +467,7 @@
             down = down.transpose(0, 2, 1, 3).reshape(PAD_ROWS, FF)
             mlp_pack = jnp.concatenate([gate_up, down], axis=-1).astype(BF16)
             packs.append((attn_pack, mlp_pack))
-        hidden = x_in.reshape(-1, D)
+        hidden = x_in.transpose(0, 2, 1)
         saved = []
         raw_attn, mlp_pack = lax.optimization_barrier((gather(packs[0][0]), packs[0][1]))
         raw_mlp = gather(mlp_pack)
@@ -402,37 +479,44 @@
             if n + 1 < layers:
                 mid, next_packs = lax.optimization_barrier((mid, packs[n + 1]))
                 raw_attn, next_mlp = gather(next_packs[0]), gather(next_packs[1])
-            out, g, u, n_t, act_t, wgu, wd = mlp_fwd(raw_mlp, mid, gains[1])
+            out, g, u, n_t, act_t, wgu, wd = mlp_fwd(raw_mlp, mid, gains[1], n + 1 == layers)
             saved.append((hidden, gains, qkv_t, o_t, wqkv_t, wo, mid, g, u, n_t, act_t, wgu, wd))
             hidden, raw_mlp = out, next_mlp
-        grad = y_cot.reshape(-1, D)
-        reduced = [None] * layers
+        grad = y_cot.transpose(0, 2, 1)
+        gate_up_sums, attn_sums, down_sums = [None] * layers, [None] * layers, [None] * layers
+        attn_grads = None
         for n in reversed(range(layers)):
             x, gains, qkv_t, o_t, wqkv_t, wo, mid, g, u, n_t, act_t, wgu, wd = saved[n]
+            pack = dw_down(act_t, grad, attn_grads)
+            pack, grad = lax.optimization_barrier((pack, grad))
+            down_sum = scatter(pack)
+            if attn_grads is None:
+                down_sums[n] = down_sum[:, :FF]
+            else:
+                attn_sums[n + 1], down_sums[n] = down_sum[:, :AW], down_sum[:, AW:AW + FF]
             dgu, dmid, dgain_mlp = mlp_bwd(grad, mid, g, u, gains[1], wgu, wd)
-            mlp_grads, dmid = lax.optimization_barrier((mlp_weight_grads(n_t, act_t, dgu, grad), dmid))
-            mlp_sum = scatter(mlp_grads)
-            grad, attn_grads = attn_bwd(dmid, x, qkv_t, o_t, gains[0], dgain_mlp, cos_t, sin_t, wqkv_t, wo)
-            attn_sum = scatter(attn_grads)
-            reduced[n] = (attn_sum, mlp_sum)
+            gate_up_grads, dmid = lax.optimization_barrier((dw_gate_up(n_t, dgu), dmid))
+            gate_up_sums[n] = scatter(gate_up_grads)
+            grad, attn_grads = attn_bwd(dmid, x, qkv_t, o_t, gains[0], dgain_mlp, cos_t, sin_t, wqkv_t, wo, GW if n > 0 else GW1)
+        attn_sums[0] = scatter(attn_grads)
 
         def collect(pick):
-            return jnp.stack([pick(*parts) for parts in reduced])
+            return jnp.stack([pick(*parts) for parts in zip(attn_sums, gate_up_sums, down_sums)])
 
         def down_rows(m):
-            return m[:, 2 * FF:].reshape(8, 8, 20, 128).transpose(2, 1, 0, 3).reshape(SHARD_FF, 1024)[:, :D]
+            return m.reshape(8, 8, 20, 128).transpose(2, 1, 0, 3).reshape(SHARD_FF, 1024)[:, :D]
 
         return (
-            hidden.reshape(shape), grad.reshape(shape),
-            collect(lambda a, m: a[:ROWS, :D]),
-            collect(lambda a, m: a[:ROWS, D:D + KV]),
-            collect(lambda a, m: a[:ROWS, D + KV:QKV]),
-            collect(lambda a, m: a[:ROWS, QKV:AW]),
-            collect(lambda a, m: m[:ROWS, :FF]),
-            collect(lambda a, m: m[:ROWS, FF:2 * FF]),
-            collect(lambda a, m: down_rows(m)),
-            collect(lambda a, m: a[ROWS, :ROWS]),
-            collect(lambda a, m: a[ROWS + 1, :ROWS]),
+            hidden.transpose(0, 2, 1), grad.transpose(0, 2, 1),
+            collect(lambda a, m, d: a[:ROWS, :D]),
+            collect(lambda a, m, d: a[:ROWS, D:D + KV]),
+            collect(lambda a, m, d: a[:ROWS, D + KV:QKV]),
+            collect(lambda a, m, d: a[:ROWS, QKV:AW]),
+            collect(lambda a, m, d: m[:ROWS, :FF]),
+            collect(lambda a, m, d: m[:ROWS, FF:2 * FF]),
+            collect(lambda a, m, d: down_rows(d)),
+            collect(lambda a, m, d: a[ROWS, :ROWS]),
+            collect(lambda a, m, d: a[ROWS + 1, :ROWS]),
         )
 
     in_specs = (shard_spec,) * 9 + (P(), P(), batch_spec, batch_spec)

time: 1430 us -> 1510 us (1.056)
  waiting for transfers between devices: 428 us -> 615 us
  local copies, waits for them, and re-layouts: 83.8 us -> 27.7 us
  Pallas kernels: 887 us -> 842 us
    reduce_scatter x4 -> x5, waiting for transfers between devices: 388 us -> 564 us  [scatter(): lax.psum_scatter(pack.reshape(DEV * PAD_ROWS, pack.shape[-1]), 'fsdp', sc...]
    unnamed x33 -> x29, local copies, waits for them, and re-layouts: 65.5 us -> 15.5 us
    pallas_call x2, Pallas kernels: 239 us -> 212 us  [attn_bwd(): pl.pallas_call(functools.partial(attn_bwd_kernel, seqs), grid=(tokens //...]
    pallas_call x2, Pallas kernels: 140 us -> 118 us  [attn_fwd(): pl.pallas_call(functools.partial(attn_fwd_kernel, seqs), grid=(tokens //...]
  transfers between devices with their start and end apart: 8 -> 9, of which waited for: 4 -> 7; matrix products, arithmetic and copies ran while one was open for 5% -> 1% of each run, Pallas kernels for 36% -> 14%
where the time goes in v2:
time: 1510 us
  Pallas kernels  842 us (56%)
  waiting for transfers between devices  615 us (41%)
  local copies, waits for them, and re-layouts  27.7 us (2%)
    reduce_scatter x5, waiting for transfers between devices, scatter(): lax.psum_scatter(pack.reshape(DEV * PAD_ROWS, pack.shape[-1]), 'fsdp', sc...  564 us
    pallas_call x2, Pallas kernels, attn_bwd(): pl.pallas_call(functools.partial(attn_bwd_kernel, seqs), grid=(tokens //...  212 us
    pallas_call x2, Pallas kernels, mlp_bwd(): pl.pallas_call(functools.partial(mlp_bwd_kernel, chunk), grid=(tokens //...  179 us
    pallas_call x2, Pallas kernels, mlp_fwd(): pl.pallas_call(functools.partial(mlp_fwd_kernel, chunk), grid=(tokens //...  177 us
    pallas_call x2, Pallas kernels, attn_fwd(): pl.pallas_call(functools.partial(attn_fwd_kernel, seqs), grid=(tokens //...  118 us
    pallas_call x2, Pallas kernels, dw_gate_up(): pl.pallas_call(dw_gate_up_kernel, grid=(2 * FF // tn,), in_specs=[const_s...  96.6 us
    pallas_call x2, Pallas kernels, dw_down(): pl.pallas_call(functools.partial(dw_down_kernel, turned), grid=(FF // tm,...  58.9 us
    all_gather x4, waiting for transfers between devices, gather(): lax.all_gather(pack, 'fsdp', axis=0, tiled=True)  47.8 us
  transfers between devices with their start and end apart: 9, of which 7 were waited for; matrix products, arithmetic and copies ran while one was open for 1% of the time, Pallas kernels for 14%

profile of v2, /device:TPU:0, one launch (start us, length us, event | category | flops | bytes accessed | tf_op | source)
XLA Modules:
  0.0 1509.1 jit_solution(15263672395063645391)
XLA Ops:
  10.6 1.2 copy.92
  11.8 1.2 copy.91
  14.8 1.6 copy.89
  18.1 38.1 %all-gather.5.cloned.1.call-done = bf16[1024,2560]{1,0:T(8,128)(2,1)} async-done(((bf16[64,2560]{1,0:T(8,128)(2,1)}), bf16[1024,2560]{1,0:T(8,128)(2,1)}) %all-gather.5.cloned.1.call-update) | async-done | bytes 5242896 | tf_op jit(solution)/shard_map/all_gather | solution.py:451
  60.7 59.9 %attn_fwd.2 = (bf16[4096,960]{1,0:T(8,128)(2,1)}, bf16[1600,4096]{1,0:T(8,128)(2,1)}, bf16[960,4096]{1,0:T(8,128)(2,1)}, bf16[1600,960]{1,0:T(8,128)(2,1)}, bf16[960,960]{1,0:T(8,128)(2,1)}) custom-call(bf16[16,64,2560]{2,1,0:T(8,128)(2,1)} %bitcast.159, bf16[16,960,256]{2,1,0:T(8,128)(2,1)} %bitcast.166, f32[1,960]{1,0:T(1,128)} %squeeze.97.gain_ref, ...), custom_call_target="tpu_custom_call" | custom-call | flops 32212254720 | bytes 32768000 | tf_op jit(solution)/shard_map/attn_fwd/pallas_call | solution.py:185
  122.3 9.7 all-gather.11.cloned.1.call-done
  132.0 88.7 %mlp_fwd.2 = (bf16[4096,960]{1,0:T(8,128)(2,1)}, f32[4096,2560]{1,0:T(8,128)}, f32[4096,2560]{1,0:T(8,128)}, bf16[960,4096]{1,0:T(8,128)(2,1)}, bf16[2560,4096]{...) custom-call(bf16[16,64,7680]{2,1,0:T(8,128)(2,1)} %bitcast.162, ...), custom_call_target="tpu_custom_call" | custom-call | flops 60397977600 | bytes 122880000 | tf_op jit(solution)/shard_map/mlp_fwd/pallas_call | solution.py:242
  222.9 58.4 %attn_fwd.3 = (bf16[4096,960]{1,0:T(8,128)(2,1)}, bf16[1600,4096]{1,0:T(8,128)(2,1)}, bf16[960,4096]{1,0:T(8,128)(2,1)}, bf16[1600,960]{1,0:T(8,128)(2,1)}, bf16[960,960]{1,0:T(8,128)(2,1)}) custom-call(bf16[16,64,2560]{2,1,0:T(8,128)(2,1)} %bitcast.161, bf16[4096,960]{1,0:T(8,128)(2,1)} %get-tuple-element.72.x_ref, f32[1,960]{1,0:T(1,128)} %squeeze.108.gain_ref, ...), custom_call_target="tpu_custom_call" | custom-call | flops 32212254720 | bytes 32768000 | tf_op jit(solution)/shard_map/attn_fwd/pallas_call | solution.py:185
  281.4 88.3 %mlp_fwd.3 = (bf16[16,960,256]{2,1,0:T(8,128)(2,1)}, f32[4096,2560]{1,0:T(8,128)}, f32[4096,2560]{1,0:T(8,128)}, bf16[960,4096]{1,0:T(8,128)(2,1)}, bf16[2560,40...) custom-call(bf16[16,64,7680]{2,1,0:T(8,128)(2,1)} %bitcast.163, ...), custom_call_target="tpu_custom_call" | custom-call | flops 60397977600 | bytes 122880000 | tf_op jit(solution)/shard_map/mlp_fwd/pallas_call | solution.py:242
  369.7 30.6 %dw_down.2 = f32[16,64,2688]{2,1,0:T(8,128)} custom-call(bf16[2560,4096]{1,0:T(8,128)(2,1)} %get-tuple-element.78.act_t, bf16[16,960,256]{2,1,0:T(8,128)(2,1)} %bitcast.164), custom_call_target="tpu_custom_call" | custom-call | flops 20132659200 | bytes 38502400 | tf_op jit(solution)/shard_map/dw_down/pallas_call | solution.py:337
  400.3 89.5 %mlp_bwd.2 = (bf16[4096,5120]{1,0:T(8,128)(2,1)}, f32[4096,960]{1,0:T(8,128)}, f32[1,960]{1,0:T(1,128)}) custom-call(bf16[16,960,256]{2,1,0:T(8,128)(2,1)} %bitcast.165, bf16[4096,960]{1,0:T(8,128)(2,1)} %get-tuple-element.73.h_ref, f32[4096,2560]{1,0:T(8,128)} %get-tuple-element.80.g_ref, f32[4096,2560]{1,0:T(8,128)} %get-tuple-element.81.u_ref, ...), custom_call_target="tpu_custom_call" | custom-call | flops 60397977600 | bytes 163840000 | tf_op jit(solution)/shard_map/mlp_bwd/pallas_call | solution.py:288
  489.8 48.3 %dw_gate_up.2 = f32[16,64,5376]{2,1,0:T(8,128)} custom-call(bf16[960,4096]{1,0:T(8,128)(2,1)} %get-tuple-element.77.n_t, bf16[4096,5120]{1,0:T(8,128)(2,1)} %get-tuple-element.84.d_ref), custom_call_target="tpu_custom_call" | custom-call | flops 40265318400 | bytes 68812800 | tf_op jit(solution)/shard_map/dw_gate_up/pallas_call | solution.py:324
  538.1 105.6 %attn_bwd.2 = (bf16[4096,960]{1,0:T(8,128)(2,1)}, f32[16,64,5376]{2,1,0:T(8,128)}) custom-call(f32[4096,960]{1,0:T(8,128)} %get-tuple-element.86.dmid_ref, bf16[4096,960]{1,0:T(8,128)(2,1)} %get-tuple-element.72.x_ref, bf16[1600,4096]{1,0:T(8,128)(2,1)} %get-tuple-element.87.qkv_ref, bf16[960,4096]{1,0:T(8,128)(2,1)} %get-tuple-element.88.o_ref, ...), custom_call_target="tpu_custom_call" | custom-call | flops 64424509440 | bytes 65536000 | tf_op jit(solution)/shard_map/attn_bwd/pallas_call | solution.py:433
  643.7 28.3 %dw_down.3 = f32[16,64,5376]{2,1,0:T(8,128)} custom-call(bf16[2560,4096]{1,0:T(8,128)(2,1)} %get-tuple-element.76.act_t, bf16[4096,960]{1,0:T(8,128)(2,1)} %get-tuple-element.94.dy_ref, f32[16,64,5376]{2,1,0:T(8,128)} %get-tuple-element.93.refs_0_), custom_call_target="tpu_custom_call", output_to_operand_aliasing={{}: (2, {})} | custom-call | flops 20132659200 | bytes 38502400 | tf_op jit(solution)/shard_map/dw_down/pallas_call | solution.py:337
  672.0 89.6 %mlp_bwd.3 = (bf16[4096,5120]{1,0:T(8,128)(2,1)}, f32[4096,960]{1,0:T(8,128)}, f32[1,960]{1,0:T(1,128)}) custom-call(bf16[4096,960]{1,0:T(8,128)(2,1)} %get-tuple-element.94.dy_ref, bf16[4096,960]{1,0:T(8,128)(2,1)} %get-tuple-element.69.h_ref, f32[4096,2560]{1,0:T(8,128)} %get-tuple-element.95.g_ref, f32[4096,2560]{1,0:T(8,128)} %get-tuple-element.96.u_ref, ...), custom_call_target="tpu_custom_call" | custom-call | flops 60397977600 | bytes 163840000 | tf_op jit(solution)/shard_map/mlp_bwd/pallas_call | solution.py:288
  761.6 48.3 %dw_gate_up.3 = f32[16,64,5376]{2,1,0:T(8,128)} custom-call(bf16[960,4096]{1,0:T(8,128)(2,1)} %get-tuple-element.75.n_t, bf16[4096,5120]{1,0:T(8,128)(2,1)} %get-tuple-element.99.d_ref), custom_call_target="tpu_custom_call" | custom-call | flops 40265318400 | bytes 68812800 | tf_op jit(solution)/shard_map/dw_gate_up/pallas_call | solution.py:324
  809.9 106.5 %attn_bwd.3 = (bf16[16,960,256]{2,1,0:T(8,128)(2,1)}, f32[16,64,2688]{2,1,0:T(8,128)}) custom-call(f32[4096,960]{1,0:T(8,128)} %get-tuple-element.101.dmid_ref, bf16[16,960,256]{2,1,0:T(8,128)(2,1)} %bitcast.167, bf16[1600,4096]{1,0:T(8,128)(2,1)} %get-tuple-element.102.qkv_ref, bf16[960,4096]{1,0:T(8,128)(2,1)} %get-tuple-element.103.o_ref, ...), custom_call_target="tpu_custom_call" | custom-call | flops 64424509440 | bytes 65536000 | tf_op jit(solution)/shard_map/attn_bwd/pallas_call | solution.py:433
  919.2 83.3 %reduce-scatter.6.cloned.1.call-done = f32[64,2688]{1,0:T(8,128)} async-done(((f32[1024,2688]{1,0:T(8,128)}), f32[64,2688]{1,0:T(8,128)}) %reduce-scatter.6.cloned.1.call-update) | async-done | bytes 688144 | tf_op jit(solution)/shard_map/reduce_scatter | solution.py:454
  1004.3 1.2 slice_bitcast_fusion.15
  1005.5 87.5 %reduce-scatter.14.cloned.1.call-done = f32[64,2688]{1,0:T(8,128)} async-done(((f32[1024,2688]{1,0:T(8,128)}), f32[64,2688]{1,0:T(8,128)}) %reduce-scatter.14.cloned.1.call-update) | async-done | bytes 688144 | tf_op jit(solution)/shard_map/reduce_scatter | solution.py:454
  1093.0 1.1 copy_bitcast_fusion
  1094.2 131.9 %reduce-scatter.10.cloned.1.call-done = f32[64,5376]{1,0:T(8,128)} async-done(((f32[1024,5376]{1,0:T(8,128)}), f32[64,5376]{1,0:T(8,128)}) %reduce-scatter.10.cloned.1.call-update) | async-done | bytes 1376272 | tf_op jit(solution)/shard_map/reduce_scatter | solution.py:454
  1226.1 1.4 slice_bitcast_fusion.5
  1227.5 131.8 %reduce-scatter.12.cloned.1.call-done = f32[64,5376]{1,0:T(8,128)} async-done(((f32[1024,5376]{1,0:T(8,128)}), f32[64,5376]{1,0:T(8,128)}) %reduce-scatter.12.cloned.1.call-update) | async-done | bytes 1376272 | tf_op jit(solution)/shard_map/reduce_scatter | solution.py:454
  1359.3 1.4 slice_bitcast_fusion.4
  1360.8 2.0 copy.72
  1362.8 129.7 %reduce-scatter.8.cloned.1.call-done = f32[64,5376]{1,0:T(8,128)} async-done(((f32[1024,5376]{1,0:T(8,128)}), f32[64,5376]{1,0:T(8,128)}) %reduce-scatter.8.cloned.1.call-update) | async-done | bytes 1376272 | tf_op jit(solution)/shard_map/reduce_scatter | solution.py:454
  1492.5 1.1 slice_bitcast_fusion.22
  1495.6 1.2 copy.70
  1496.8 1.2 copy.67
  1498.1 2.0 copy.71
  1501.2 1.1 pad_maximum_fusion.2
  (99 shorter events, 23.0 us)
Async XLA Ops:
  7.2 49.0 %all-gather.5.cloned.1.call-start = ((), (), s32[]{:S(2)}) async-start(), calls=%async_computation.5 | async-start | bytes 5570560 | tf_op jit(solution)/shard_map/all_gather | solution.py:451
  13.1 1.5 copy-start.2
  14.5 1.9 copy-start.1
  14.5 117.5 %all-gather.11.cloned.1.call-start = ((), (), s32[]{:S(2)}) async-start(), calls=%async_computation.8 | async-start | bytes 16711680 | tf_op jit(solution)/shard_map/all_gather | solution.py:451
  17.0 39.4 %copy-start.3 = (f32[256,32]{0,1:T(8,128)S(1)}, f32[256,32]{0,1:T(8,128)}, u32[]{:S(2)}) copy-start(f32[256,32]{0,1:T(8,128)} %param.22) | copy-start | bytes 98308
  17.1 40.1 %copy-start.4 = (f32[256,32]{0,1:T(8,128)S(1)}, f32[256,32]{0,1:T(8,128)}, u32[]{:S(2)}) copy-start(f32[256,32]{0,1:T(8,128)} %param.23) | copy-start | bytes 98308
  56.2 164.5 %all-gather.9.cloned.1.call-start = ((), (), s32[]{:S(2)}) async-start(), calls=%async_computation.7 | async-start | bytes 5570560 | tf_op jit(solution)/shard_map/all_gather | solution.py:451
  120.6 160.8 %all-gather.7.cloned.1.call-start = ((), (), s32[]{:S(2)}) async-start(), calls=%async_computation.6 | async-start | bytes 16711680 | tf_op jit(solution)/shard_map/all_gather | solution.py:451
  121.2 881.3 %reduce-scatter.6.cloned.1.call-start = ((), (), s32[]{:S(2)}) async-start(), calls=%async_computation.9 | async-start | bytes 11698176 | tf_op jit(solution)/shard_map/reduce_scatter | solution.py:454
  916.4 176.6 %reduce-scatter.14.cloned.1.call-start = ((), (), s32[]{:S(2)}) async-start(), calls=%async_computation.13 | async-start | bytes 11698176 | tf_op jit(solution)/shard_map/reduce_scatter | solution.py:454
  917.0 309.2 %reduce-scatter.10.cloned.1.call-start = ((), (), s32[]{:S(2)}) async-start(), calls=%async_computation.11 | async-start | bytes 23396352 | tf_op jit(solution)/shard_map/reduce_scatter | solution.py:454
  917.7 441.6 %reduce-scatter.12.cloned.1.call-start = ((), (), s32[]{:S(2)}) async-start(), calls=%async_computation.12 | async-start | bytes 23396352 | tf_op jit(solution)/shard_map/reduce_scatter | solution.py:454
  918.5 574.0 %reduce-scatter.8.cloned.1.call-start = ((), (), s32[]{:S(2)}) async-start(), calls=%async_computation.10 | async-start | bytes 23396352 | tf_op jit(solution)/shard_map/reduce_scatter | solution.py:454
  1492.5 2.8 copy-start
Sparse Core Ops, SparseCore 0:
  14.6 41.5 all-gather.4
  59.0 72.9 all-gather.10
  134.8 38.7 all-gather.8
  176.3 72.9 all-gather.6
  916.5 85.9 reduce-scatter.5
  1007.2 85.7 reduce-scatter.13
  1097.9 128.2 reduce-scatter.9
  1231.0 128.2 reduce-scatter.11
  1364.2 128.2 reduce-scatter.7
